TPU v7x, 512 devices: a whole 4x4x16 slice. The times are simulated.
512 devices in a mesh: gx: 16 (over y, x), gy: 16 (over z), gz: 2 (over core).
Axes of the slice: x: 4, y: 4, z: 16, core: 2. Of those that a mesh axis runs over, the one named last changes fastest.
Arguments:
- forcing: float32 [256, 1024, 256], P('gx', 'gy', 'gz'), may hold values from -6 to 6
- conductivity: float32 [32, 128, 32], P('gx', 'gy', 'gz'), may hold values from 0.5 to 4
- lower_bound: float32 [1], replicated, may hold values from 0.1 to 0.3
- upper_bound: float32 [1], replicated, may hold values from 1.6 to 2.4
Outputs:
- solution: float32 [256, 1024, 256], P('gx', 'gy', 'gz')
- ratios: float32 [2], replicated
All inputs are finite; a program needn't handle non-finite values.
Results may differ from a plain program's by a relative error of at most 0.00012.
Values sent between devices are 32-bit elements; how exact they have to be, the bound alone decides.
A program may use at most 64 MiB of HBM per device.

v0:
```python
import functools

import jax
import jax.numpy as jnp
import numpy as np
from jax import lax
from jax.sharding import Mesh
from jax.sharding import PartitionSpec as P

SWEEPS = 2
GX = ("gx_0", "gx_1")
GX_GY_GZ = ("gx_0", "gx_1", "gy", "gz")


gll_inner = [0.20929921790247888, 0.5917001814331423, 0.8717401485096066]


def extended(block, sides, width):
    for axis, dim in sides:
        count = lax.axis_size(axis)
        forward = [(i, i + 1) for i in range(count - 1)]
        backward = [(target, source) for source, target in forward]
        low = lax.ppermute(
            lax.slice_in_dim(block, block.shape[dim] - width, None, axis=dim), axis, forward
        )
        high = lax.ppermute(lax.slice_in_dim(block, 0, width, axis=dim), axis, backward)
        block = jnp.concatenate([low, block, high], axis=dim)
    return block


def by_axis(array, axes):
    return functools.reduce(lax.psum, axes, array)


def gll_tables():
    degree_val = 7
    points = np.array(
        [
            -1.0,
            -gll_inner[2],
            -gll_inner[1],
            -gll_inner[0],
            gll_inner[0],
            gll_inner[1],
            gll_inner[2],
            1.0,
        ]
    )
    previous = np.ones(8)
    values = points * 1.0
    for order in range(1, degree_val):
        following = ((2.0 * order + 1.0) * points * values - order * previous) / (order + 1.0)
        previous = values
        values = following
    weights = 2.0 / (degree_val * (degree_val + 1) * values**2)
    differ = points[:, None] - points[None, :]
    safe_gap = np.where(differ == 0.0, 1.0, differ)
    derivative = np.where(differ == 0.0, 0.0, values[:, None] / values[None, :] / safe_gap)
    corner_val = degree_val * (degree_val + 1) / 4.0
    ends_vec = np.concatenate([np.array([-corner_val]), np.zeros(6), np.array([corner_val])])
    index_row = np.arange(8)
    derivative = derivative + np.where(
        index_row[:, None] == index_row[None, :], ends_vec[None, :], 0.0
    )
    stiffness = derivative.T @ (weights[:, None] * derivative)
    return (weights, stiffness)


def edge_masks(length):
    positions = jnp.arange(length) % 8
    return ((positions == 0).astype(jnp.float32), (positions == 7).astype(jnp.float32))


def pair_sum(padded, which_axis, masks):
    is_first, is_last = masks
    length = padded.shape[which_axis] - 2
    centre = lax.slice_in_dim(padded, 1, length + 1, axis=which_axis)
    upper_side = lax.slice_in_dim(padded, 2, length + 2, axis=which_axis)
    lower_side = lax.slice_in_dim(padded, 0, length, axis=which_axis)
    view_shape = [1] * padded.ndim
    view_shape[which_axis] = length
    return (
        centre
        + jnp.reshape(is_last, view_shape) * upper_side
        + jnp.reshape(is_first, view_shape) * lower_side
    )


def inside(global_pos, length):
    return ((global_pos > 0) & (global_pos < length - 1)).astype(jnp.float32)


def per_device(forcing, conductivity, lower_bound, upper_bound):
    weights, stiffness = gll_tables()
    weights = jnp.asarray(weights, jnp.float32)
    stiffness = jnp.asarray(stiffness, jnp.float32)
    size_x, size_y, size_z = forcing.shape
    rims_x = edge_masks(size_x)
    rims_y = edge_masks(size_y)
    rims_z = edge_masks(size_z)
    keep_x = inside(lax.axis_index(GX) * size_x + jnp.arange(size_x), lax.axis_size(GX) * size_x)
    keep_y = inside(
        lax.axis_index("gy") * size_y + jnp.arange(size_y), lax.axis_size("gy") * size_y
    )
    keep_z = inside(
        lax.axis_index("gz") * size_z + jnp.arange(size_z), lax.axis_size("gz") * size_z
    )
    dirichlet = keep_x[:, None, None] * keep_y[None, :, None] * keep_z[None, None, :]
    mult_x = 1.0 + rims_x[0] + rims_x[1]
    mult_y = 1.0 + rims_y[0] + rims_y[1]
    mult_z = 1.0 + rims_z[0] + rims_z[1]
    inv_mult = 1.0 / (mult_x[:, None, None] * mult_y[None, :, None] * mult_z[None, None, :])
    block_x = jnp.kron(jnp.eye(size_x // 8, dtype=jnp.float32), stiffness)
    block_y = jnp.kron(jnp.eye(size_y // 8, dtype=jnp.float32), stiffness)
    block_z = jnp.kron(jnp.eye(size_z // 8, dtype=jnp.float32), stiffness)
    wgt_x = jnp.tile(weights, size_x // 8)[:, None, None]
    wgt_y = jnp.tile(weights, size_y // 8)[None, :, None]
    wgt_z = jnp.tile(weights, size_z // 8)[None, None, :]
    stiff_diag = jnp.diagonal(stiffness)
    diag_x = jnp.tile(stiff_diag, size_x // 8)[:, None, None]
    diag_y = jnp.tile(stiff_diag, size_y // 8)[None, :, None]
    diag_z = jnp.tile(stiff_diag, size_z // 8)[None, None, :]
    cond_nodes = jnp.repeat(jnp.repeat(jnp.repeat(conductivity, 8, axis=0), 8, axis=1), 8, axis=2)
    high = lax.Precision.HIGHEST

    def assemble(stacked):
        padded = extended(stacked, ((GX, 1),), 1)
        stacked = pair_sum(padded, 1, rims_x)
        padded = extended(stacked, (("gy", 2),), 1)
        stacked = pair_sum(padded, 2, rims_y)
        padded = extended(stacked, (("gz", 3),), 1)
        stacked = pair_sum(padded, 3, rims_z)
        return stacked

    def local_apply(field):
        along_x = jnp.dot(block_x, field.reshape(size_x, -1), precision=high).reshape(field.shape)
        along_y = jnp.einsum("ayz,yq->aqz", field, block_y, precision=high)
        along_z = jnp.dot(field.reshape(-1, size_z), block_z, precision=high).reshape(field.shape)
        return cond_nodes * (
            along_x * wgt_y * wgt_z + wgt_x * along_y * wgt_z + wgt_x * wgt_y * along_z
        )

    def operate(field):
        return dirichlet * assemble(local_apply(field)[None])[0]

    diag_local = cond_nodes * (
        diag_x * wgt_y * wgt_z + wgt_x * diag_y * wgt_z + wgt_x * wgt_y * diag_z
    )
    both = assemble(jnp.stack([forcing, diag_local]))
    source = dirichlet * both[0]
    inverse = dirichlet / both[1]
    centre_val = (upper_bound[0] + lower_bound[0]) / 2.0
    half_width = (upper_bound[0] - lower_bound[0]) / 2.0
    rho_first = half_width / centre_val
    rho_second = 1.0 / (2.0 * centre_val / half_width - rho_first)
    source_part = jnp.sum(source * source * inv_mult)
    source_sq = by_axis(source_part, GX_GY_GZ)
    solution = jnp.zeros_like(source)
    residual = source
    ratios = []
    for sweep in range(SWEEPS):
        update = inverse * residual / centre_val
        solution = solution + update
        residual = residual - operate(update)
        update = (
            rho_second * rho_first * update + 2.0 * rho_second / half_width * inverse * residual
        )
        solution = solution + update
        residual = residual - operate(update)
        local_part = jnp.sum(residual * residual * inv_mult)
        summed = by_axis(local_part, GX_GY_GZ)
        ratios.append(jnp.sqrt(summed / source_sq))
    result_ratios = jnp.stack(ratios)
    return (solution, result_ratios)


def solution(mesh):
    torus = Mesh(
        mesh.devices.reshape(4, 4, mesh.shape["gy"], mesh.shape["gz"]), ("gx_0", "gx_1", "gy", "gz")
    )
    in_specs = (P(GX, "gy", "gz"), P(GX, "gy", "gz"), P(), P())
    out_specs = (P(GX, "gy", "gz"), P())
    return jax.shard_map(
        per_device, mesh=torus, in_specs=in_specs, out_specs=out_specs, check_vma=False
    )
```

profile of v0, /device:TPU:1, one launch (start us, length us, event | category | flops | bytes accessed | tf_op | source)
XLA Modules:
  0.0 239.5 jit_solution(4381099032714966543)
XLA Ops:
  7.8 4.6 %collective-permute-start.1 = (f32[2,1,64,128]{3,1,2,0:T(1,128)S(1)}, f32[2,1,64,128]{3,1,2,0:T(1,128)S(1)}, u32[]{:S(2)}, u32[]{:S(2)}) collective-permute-start(f32[2,1,64,128]{3,1,2,0:T(1,128)S(1)} %get-tuple-element.42), channel_id=1, source_target_pairs={{0,32},{32,64},{64,96},{96,128},{128,160},{160,192},{192,224},{224... | collective-permute-start | bytes 196616 | tf_op jit(solution)/shard_map/ppermute | solution.py:23
  16.2 4.4 %collective-permute-start.3 = (f32[2,16,1,128]{3,1,2,0:T(8,128)S(1)}, f32[2,16,1,128]{3,1,2,0:T(8,128)S(1)}, u32[]{:S(2)}, u32[]{:S(2)}) collective-permute-start(f32[2,16,1,128]{3,1,2,0:T(8,128)S(1)} %get-tuple-element.40), channel_id=1, source_target_pairs={{0,2},{2,4},{4,6},{6,8},{8,10},{10,12},{12,14},{14,16},{16,18},{18... | collective-permute-start | bytes 49160 | tf_op jit(solution)/shard_map/ppermute | solution.py:23
  25.1 9.4 %collective-permute-start.4 = (f32[2,16,64,1]{2,1,3,0:T(8,128)S(1)}, f32[2,16,64,1]{2,1,3,0:T(8,128)S(1)}, u32[]{:S(2)}, u32[]{:S(2)}) collective-permute-start(f32[2,16,64,1]{2,1,3,0:T(8,128)S(1)} %copy.142), channel_id=1, source_target_pairs={{1,0},{3,2},{5,4},{7,6},{9,8},{11,10},{13,12},{15,14},{17,16},{19,... | collective-permute-start | bytes 24584 | tf_op jit(solution)/shard_map/ppermute | solution.py:26
  44.1 2.4 %fusion.23 = f32[2,16,64,128]{3,1,2,0:T(8,128)S(1)} fusion(f32[2,16,64,128]{3,1,2,0:T(8,128)S(1)} %fusion.27, f32[2,16,64,1]{3,1,2,0:T(8,128)} %copy.145, f32[2,16,64,1]{3,1,2,0:T(8,128)} %copy.143, f32[128]{0:T(128)S(1)} %get-tuple-element.75, f32[128]{0:T(128)S(1)} %get-tuple-element.76), kind=kLoop, calls=%fused_computation.49 | loop fusion | flops 1572864 | bytes 2114560 | tf_op jit(solution)/shard_map/add | solution.py:83
  51.9 4.4 %collective-permute-start.7 = (f32[1,1,64,128]{3,1,2,0:T(1,128)S(1)}, f32[1,1,64,128]{3,1,2,0:T(1,128)S(1)}, u32[]{:S(2)}, u32[]{:S(2)}) collective-permute-start(f32[1,1,64,128]{3,1,2,0:T(1,128)S(1)} %get-tuple-element.66), channel_id=1, source_target_pairs={{0,32},{32,64},{64,96},{96,128},{128,160},{160,192},{192,224},{224... | collective-permute-start | bytes 98312 | tf_op jit(solution)/shard_map/ppermute | solution.py:23
  58.8 4.6 %collective-permute-start.9 = (f32[1,16,1,128]{3,1,2,0:T(8,128)S(1)}, f32[1,16,1,128]{3,1,2,0:T(8,128)S(1)}, u32[]{:S(2)}, u32[]{:S(2)}) collective-permute-start(f32[1,16,1,128]{3,1,2,0:T(8,128)S(1)} %get-tuple-element.64), channel_id=1, source_target_pairs={{0,2},{2,4},{4,6},{6,8},{8,10},{10,12},{12,14},{14,16},{16,18},{18... | collective-permute-start | bytes 24584 | tf_op jit(solution)/shard_map/ppermute | solution.py:23
  65.3 5.5 %collective-permute-start.10 = (f32[1,16,64,1]{3,1,2,0:T(8,128)}, f32[1,16,64,1]{3,1,2,0:T(8,128)}, u32[]{:S(2)}, u32[]{:S(2)}) collective-permute-start(f32[1,16,64,1]{3,1,2,0:T(8,128)} %get-tuple-element.61), channel_id=1, source_target_pairs={{1,0},{3,2},{5,4},{7,6},{9,8},{11,10},{13,12},{15,14},{17,16},{19,... | collective-permute-start | bytes 12296 | tf_op jit(solution)/shard_map/ppermute | solution.py:26
  78.0 2.4 %fusion.14 = f32[16,64,128]{2,0,1:T(8,128)S(1)} fusion(f32[16,16,1]{1,0,2:T(8,128)S(1)} %reshape.587, f32[64,16,128]{2,0,1:T(8,128)S(1)} %fusion.115, f32[128]{0:T(128)S(1)} %mul.1062, f32[16]{0:T(128)S(1)} %mul.1065, f32[64]{0:T(128)S(1)} %mul.1058, f32[]{:T(128)S(6)} %div.119, f32[]{:T(128)S(6)} %mul.1092, f32[]{:T(128)S(6)} %div.111, ...), kind=kOutput, calls=%fused_computation.37 | convolution fusion | flops 27262976 | bytes 3180364 | tf_op jit(solution)/shard_map/dot_general | solution.py:136
  82.4 4.6 %collective-permute-start.13 = (f32[1,1,64,128]{3,1,2,0:T(1,128)S(1)}, f32[1,1,64,128]{3,1,2,0:T(1,128)S(1)}, u32[]{:S(2)}, u32[]{:S(2)}) collective-permute-start(f32[1,1,64,128]{3,1,2,0:T(1,128)S(1)} %get-tuple-element.60), channel_id=1, source_target_pairs={{0,32},{32,64},{64,96},{96,128},{128,160},{160,192},{192,224},{224... | collective-permute-start | bytes 98312 | tf_op jit(solution)/shard_map/ppermute | solution.py:23
  89.5 4.5 %collective-permute-start.15 = (f32[1,16,1,128]{3,1,2,0:T(8,128)S(1)}, f32[1,16,1,128]{3,1,2,0:T(8,128)S(1)}, u32[]{:S(2)}, u32[]{:S(2)}) collective-permute-start(f32[1,16,1,128]{3,1,2,0:T(8,128)S(1)} %get-tuple-element.58), channel_id=1, source_target_pairs={{0,2},{2,4},{4,6},{6,8},{8,10},{10,12},{12,14},{14,16},{16,18},{18... | collective-permute-start | bytes 24584 | tf_op jit(solution)/shard_map/ppermute | solution.py:23
  95.2 3.8 %collective-permute-start.16 = (f32[1,16,64,1]{3,1,2,0:T(8,128)S(1)}, f32[1,16,64,1]{3,1,2,0:T(8,128)S(1)}, u32[]{:S(2)}, u32[]{:S(2)}) collective-permute-start(f32[1,16,64,1]{3,1,2,0:T(8,128)S(1)} %get-tuple-element.55), channel_id=1, source_target_pairs={{1,0},{3,2},{5,4},{7,6},{9,8},{11,10},{13,12},{15,14},{17,16},{19,... | collective-permute-start | bytes 12296 | tf_op jit(solution)/shard_map/ppermute | solution.py:26
  100.5 2.3 collective-permute-done.17
  104.4 3.0 %fusion.9 = f32[16,64,128]{2,0,1:T(8,128)S(1)} fusion(f32[16,16,1]{1,0,2:T(8,128)S(1)} %reshape.587, f32[64,16,128]{2,0,1:T(8,128)S(1)} %fusion.112, f32[128]{0:T(128)S(1)} %mul.1062, f32[16]{0:T(128)S(1)} %mul.1065, f32[64]{0:T(128)S(1)} %mul.1058, f32[]{:T(128)S(6)} %div.111, f32[2,8,64,128]{3,2,1,0:T(8,128)S(1)} %bitcast.285, ...), kind=kOutput, calls=%fused_computation.30 | convolution fusion | flops 27000832 | bytes 3704644 | tf_op jit(solution)/shard_map/dot_general | solution.py:136
  109.4 4.6 %collective-permute-start.19 = (f32[1,1,64,128]{3,1,2,0:T(1,128)S(1)}, f32[1,1,64,128]{3,1,2,0:T(1,128)S(1)}, u32[]{:S(2)}, u32[]{:S(2)}) collective-permute-start(f32[1,1,64,128]{3,1,2,0:T(1,128)S(1)} %get-tuple-element.54), channel_id=1, source_target_pairs={{0,32},{32,64},{64,96},{96,128},{128,160},{160,192},{192,224},{224... | collective-permute-start | bytes 98312 | tf_op jit(solution)/shard_map/ppermute | solution.py:23
  116.5 4.5 %collective-permute-start.21 = (f32[1,16,1,128]{3,1,2,0:T(8,128)S(1)}, f32[1,16,1,128]{3,1,2,0:T(8,128)S(1)}, u32[]{:S(2)}, u32[]{:S(2)}) collective-permute-start(f32[1,16,1,128]{3,1,2,0:T(8,128)S(1)} %get-tuple-element.52), channel_id=1, source_target_pairs={{0,2},{2,4},{4,6},{6,8},{8,10},{10,12},{12,14},{14,16},{16,18},{18... | collective-permute-start | bytes 24584 | tf_op jit(solution)/shard_map/ppermute | solution.py:23
  122.2 3.8 %collective-permute-start.22 = (f32[1,16,64,1]{3,1,2,0:T(8,128)S(1)}, f32[1,16,64,1]{3,1,2,0:T(8,128)S(1)}, u32[]{:S(2)}, u32[]{:S(2)}) collective-permute-start(f32[1,16,64,1]{3,1,2,0:T(8,128)S(1)} %get-tuple-element.49), channel_id=1, source_target_pairs={{1,0},{3,2},{5,4},{7,6},{9,8},{11,10},{13,12},{15,14},{17,16},{19,... | collective-permute-start | bytes 12296 | tf_op jit(solution)/shard_map/ppermute | solution.py:26
  131.4 3.6 %fusion.4 = f32[16,64,128]{2,0,1:T(8,128)S(1)} fusion(f32[16,16,1]{1,0,2:T(8,128)S(1)} %reshape.587, f32[64,16,128]{2,0,1:T(8,128)S(1)} %fusion.109, f32[128]{0:T(128)S(1)} %mul.1062, f32[16]{0:T(128)S(1)} %mul.1065, f32[64]{0:T(128)S(1)} %mul.1058, f32[2,8,64,128]{3,2,1,0:T(8,128)S(1)} %bitcast.287, f32[2,8,64,128]{3,2,1,0:T(8,128)S(1)} %bitcast.281, ...), kind=kOutput, calls=%fused_computation.23 | convolution fusion | flops 27787264 | bytes 4228940 | tf_op jit(solution)/shard_map/dot_general | solution.py:136
  136.9 4.6 %collective-permute-start.25 = (f32[1,1,64,128]{3,1,2,0:T(1,128)S(1)}, f32[1,1,64,128]{3,1,2,0:T(1,128)S(1)}, u32[]{:S(2)}, u32[]{:S(2)}) collective-permute-start(f32[1,1,64,128]{3,1,2,0:T(1,128)S(1)} %get-tuple-element.48), channel_id=1, source_target_pairs={{0,32},{32,64},{64,96},{96,128},{128,160},{160,192},{192,224},{224... | collective-permute-start | bytes 98312 | tf_op jit(solution)/shard_map/ppermute | solution.py:23
  144.0 4.5 %collective-permute-start.27 = (f32[1,16,1,128]{3,1,2,0:T(8,128)S(1)}, f32[1,16,1,128]{3,1,2,0:T(8,128)S(1)}, u32[]{:S(2)}, u32[]{:S(2)}) collective-permute-start(f32[1,16,1,128]{3,1,2,0:T(8,128)S(1)} %get-tuple-element.46), channel_id=1, source_target_pairs={{0,2},{2,4},{4,6},{6,8},{8,10},{10,12},{12,14},{14,16},{16,18},{18... | collective-permute-start | bytes 24584 | tf_op jit(solution)/shard_map/ppermute | solution.py:23
  149.7 3.8 %collective-permute-start.28 = (f32[1,16,64,1]{3,1,2,0:T(8,128)S(1)}, f32[1,16,64,1]{3,1,2,0:T(8,128)S(1)}, u32[]{:S(2)}, u32[]{:S(2)}) collective-permute-start(f32[1,16,64,1]{3,1,2,0:T(8,128)S(1)} %get-tuple-element.43), channel_id=1, source_target_pairs={{1,0},{3,2},{5,4},{7,6},{9,8},{11,10},{13,12},{15,14},{17,16},{19,... | collective-permute-start | bytes 12296 | tf_op jit(solution)/shard_map/ppermute | solution.py:26
  158.7 19.1 %all-reduce.2 = (f32[]{:T(128)}, f32[]{:T(128)}, f32[]{:T(128)}) all-reduce(f32[]{:T(128)} %get-tuple-element.13, f32[]{:T(128)} %get-tuple-element.14, f32[]{:T(128)} %get-tuple-element.12), channel_id=1, replica_groups=mesh['gx_0'=4,'gx_1'=4,'gy'=16,'gz'=2] {'gx_0'}, use_global_device_ids=true, to_apply=%region_11.12 | all-reduce | flops 3 | bytes 24 | tf_op jit(solution)/shard_map/psum | solution.py:32
  177.8 6.6 %all-reduce.1 = (f32[]{:T(128)}, f32[]{:T(128)}, f32[]{:T(128)}) all-reduce(f32[]{:T(128)} %get-tuple-element.21, f32[]{:T(128)} %get-tuple-element.22, f32[]{:T(128)} %get-tuple-element.23), channel_id=1, replica_groups=mesh['gx_0'=4,'gx_1'=4,'gy'=16,'gz'=2] {'gx_1'}, use_global_device_ids=true, to_apply=%region_12.13 | all-reduce | flops 3 | bytes 24 | tf_op jit(solution)/shard_map/psum | solution.py:32
  184.5 36.5 %all-reduce = (f32[]{:T(128)}, f32[]{:T(128)}, f32[]{:T(128)}) all-reduce(f32[]{:T(128)} %get-tuple-element.18, f32[]{:T(128)} %get-tuple-element.19, f32[]{:T(128)} %get-tuple-element.20), channel_id=1, replica_groups=mesh['gx_0'=4,'gx_1'=4,'gy'=16,'gz'=2] {'gy'}, use_global_device_ids=true, to_apply=%region_13.14 | all-reduce | flops 3 | bytes 24 | tf_op jit(solution)/shard_map/psum | solution.py:32
  220.9 13.9 %all-reduce.3 = (f32[]{:T(128)}, f32[]{:T(128)}, f32[]{:T(128)}) all-reduce(f32[]{:T(128)} %get-tuple-element.15, f32[]{:T(128)} %get-tuple-element.16, f32[]{:T(128)} %get-tuple-element.17), channel_id=1, replica_groups=mesh['gx_0'=4,'gx_1'=4,'gy'=16,'gz'=2] {'gz'}, use_global_device_ids=true, to_apply=%region_14.15 | all-reduce | flops 3 | bytes 24 | tf_op jit(solution)/shard_map/psum | solution.py:32
  (163 shorter events, 72.4 us)
Async XLA Ops:
  6.5 8.0 %collective-permute-start = (f32[2,1,64,128]{3,1,2,0:T(1,128)S(1)}, f32[2,1,64,128]{3,1,2,0:T(1,128)S(1)}, u32[]{:S(2)}, u32[]{:S(2)}) collective-permute-start(f32[2,1,64,128]{3,1,2,0:T(1,128)S(1)} %get-tuple-element.41), channel_id=1, source_target_pairs={{32,0},{64,32},{96,64},{128,96},{160,128},{192,160},{224,192},{256... | collective-permute-start | bytes 196616 | tf_op jit(solution)/shard_map/ppermute | solution.py:26
  7.8 6.7 %collective-permute-start.1 = (f32[2,1,64,128]{3,1,2,0:T(1,128)S(1)}, f32[2,1,64,128]{3,1,2,0:T(1,128)S(1)}, u32[]{:S(2)}, u32[]{:S(2)}) collective-permute-start(f32[2,1,64,128]{3,1,2,0:T(1,128)S(1)} %get-tuple-element.42), channel_id=1, source_target_pairs={{0,32},{32,64},{64,96},{96,128},{128,160},{160,192},{192,224},{224... | collective-permute-start | bytes 196616 | tf_op jit(solution)/shard_map/ppermute | solution.py:23
  14.9 5.7 %collective-permute-start.2 = (f32[2,16,1,128]{3,1,2,0:T(8,128)S(1)}, f32[2,16,1,128]{3,1,2,0:T(8,128)S(1)}, u32[]{:S(2)}, u32[]{:S(2)}) collective-permute-start(f32[2,16,1,128]{3,1,2,0:T(8,128)S(1)} %get-tuple-element.39), channel_id=1, source_target_pairs={{2,0},{4,2},{6,4},{8,6},{10,8},{12,10},{14,12},{16,14},{18,16},{20... | collective-permute-start | bytes 49160 | tf_op jit(solution)/shard_map/ppermute | solution.py:26
  25.1 16.0 %collective-permute-start.4 = (f32[2,16,64,1]{2,1,3,0:T(8,128)S(1)}, f32[2,16,64,1]{2,1,3,0:T(8,128)S(1)}, u32[]{:S(2)}, u32[]{:S(2)}) collective-permute-start(f32[2,16,64,1]{2,1,3,0:T(8,128)S(1)} %copy.142), channel_id=1, source_target_pairs={{1,0},{3,2},{5,4},{7,6},{9,8},{11,10},{13,12},{15,14},{17,16},{19,... | collective-permute-start | bytes 24584 | tf_op jit(solution)/shard_map/ppermute | solution.py:26
  36.2 6.4 %collective-permute-start.5 = (f32[2,16,64,1]{2,1,3,0:T(8,128)S(1)}, f32[2,16,64,1]{2,1,3,0:T(8,128)S(1)}, u32[]{:S(2)}, u32[]{:S(2)}) collective-permute-start(f32[2,16,64,1]{2,1,3,0:T(8,128)S(1)} %copy.144), channel_id=1, source_target_pairs={{0,1},{2,3},{4,5},{6,7},{8,9},{10,11},{12,13},{14,15},{16,17},{18,... | collective-permute-start | bytes 24584 | tf_op jit(solution)/shard_map/ppermute | solution.py:23
  50.6 5.7 %collective-permute-start.6 = (f32[1,1,64,128]{3,1,2,0:T(1,128)S(1)}, f32[1,1,64,128]{3,1,2,0:T(1,128)S(1)}, u32[]{:S(2)}, u32[]{:S(2)}) collective-permute-start(f32[1,1,64,128]{3,1,2,0:T(1,128)S(1)} %get-tuple-element.65), channel_id=1, source_target_pairs={{32,0},{64,32},{96,64},{128,96},{160,128},{192,160},{224,192},{256... | collective-permute-start | bytes 98312 | tf_op jit(solution)/shard_map/ppermute | solution.py:26
  51.9 5.4 %collective-permute-start.7 = (f32[1,1,64,128]{3,1,2,0:T(1,128)S(1)}, f32[1,1,64,128]{3,1,2,0:T(1,128)S(1)}, u32[]{:S(2)}, u32[]{:S(2)}) collective-permute-start(f32[1,1,64,128]{3,1,2,0:T(1,128)S(1)} %get-tuple-element.66), channel_id=1, source_target_pairs={{0,32},{32,64},{64,96},{96,128},{128,160},{160,192},{192,224},{224... | collective-permute-start | bytes 98312 | tf_op jit(solution)/shard_map/ppermute | solution.py:23
  57.5 5.9 %collective-permute-start.8 = (f32[1,16,1,128]{3,1,2,0:T(8,128)S(1)}, f32[1,16,1,128]{3,1,2,0:T(8,128)S(1)}, u32[]{:S(2)}, u32[]{:S(2)}) collective-permute-start(f32[1,16,1,128]{3,1,2,0:T(8,128)S(1)} %get-tuple-element.63), channel_id=1, source_target_pairs={{2,0},{4,2},{6,4},{8,6},{10,8},{12,10},{14,12},{16,14},{18,16},{20... | collective-permute-start | bytes 24584 | tf_op jit(solution)/shard_map/ppermute | solution.py:26
  58.8 5.3 %collective-permute-start.9 = (f32[1,16,1,128]{3,1,2,0:T(8,128)S(1)}, f32[1,16,1,128]{3,1,2,0:T(8,128)S(1)}, u32[]{:S(2)}, u32[]{:S(2)}) collective-permute-start(f32[1,16,1,128]{3,1,2,0:T(8,128)S(1)} %get-tuple-element.64), channel_id=1, source_target_pairs={{0,2},{2,4},{4,6},{6,8},{8,10},{10,12},{12,14},{14,16},{16,18},{18... | collective-permute-start | bytes 24584 | tf_op jit(solution)/shard_map/ppermute | solution.py:23
  65.3 7.2 %collective-permute-start.10 = (f32[1,16,64,1]{3,1,2,0:T(8,128)}, f32[1,16,64,1]{3,1,2,0:T(8,128)}, u32[]{:S(2)}, u32[]{:S(2)}) collective-permute-start(f32[1,16,64,1]{3,1,2,0:T(8,128)} %get-tuple-element.61), channel_id=1, source_target_pairs={{1,0},{3,2},{5,4},{7,6},{9,8},{11,10},{13,12},{15,14},{17,16},{19,... | collective-permute-start | bytes 12296 | tf_op jit(solution)/shard_map/ppermute | solution.py:26
  81.1 5.9 %collective-permute-start.12 = (f32[1,1,64,128]{3,1,2,0:T(1,128)S(1)}, f32[1,1,64,128]{3,1,2,0:T(1,128)S(1)}, u32[]{:S(2)}, u32[]{:S(2)}) collective-permute-start(f32[1,1,64,128]{3,1,2,0:T(1,128)S(1)} %get-tuple-element.59), channel_id=1, source_target_pairs={{32,0},{64,32},{96,64},{128,96},{160,128},{192,160},{224,192},{256... | collective-permute-start | bytes 98312 | tf_op jit(solution)/shard_map/ppermute | solution.py:26
  82.4 5.6 %collective-permute-start.13 = (f32[1,1,64,128]{3,1,2,0:T(1,128)S(1)}, f32[1,1,64,128]{3,1,2,0:T(1,128)S(1)}, u32[]{:S(2)}, u32[]{:S(2)}) collective-permute-start(f32[1,1,64,128]{3,1,2,0:T(1,128)S(1)} %get-tuple-element.60), channel_id=1, source_target_pairs={{0,32},{32,64},{64,96},{96,128},{128,160},{160,192},{192,224},{224... | collective-permute-start | bytes 98312 | tf_op jit(solution)/shard_map/ppermute | solution.py:23
  88.2 5.8 %collective-permute-start.14 = (f32[1,16,1,128]{3,1,2,0:T(8,128)S(1)}, f32[1,16,1,128]{3,1,2,0:T(8,128)S(1)}, u32[]{:S(2)}, u32[]{:S(2)}) collective-permute-start(f32[1,16,1,128]{3,1,2,0:T(8,128)S(1)} %get-tuple-element.57), channel_id=1, source_target_pairs={{2,0},{4,2},{6,4},{8,6},{10,8},{12,10},{14,12},{16,14},{18,16},{20... | collective-permute-start | bytes 24584 | tf_op jit(solution)/shard_map/ppermute | solution.py:26
  89.5 5.3 %collective-permute-start.15 = (f32[1,16,1,128]{3,1,2,0:T(8,128)S(1)}, f32[1,16,1,128]{3,1,2,0:T(8,128)S(1)}, u32[]{:S(2)}, u32[]{:S(2)}) collective-permute-start(f32[1,16,1,128]{3,1,2,0:T(8,128)S(1)} %get-tuple-element.58), channel_id=1, source_target_pairs={{0,2},{2,4},{4,6},{6,8},{8,10},{10,12},{12,14},{14,16},{16,18},{18... | collective-permute-start | bytes 24584 | tf_op jit(solution)/shard_map/ppermute | solution.py:23
  95.2 5.3 %collective-permute-start.16 = (f32[1,16,64,1]{3,1,2,0:T(8,128)S(1)}, f32[1,16,64,1]{3,1,2,0:T(8,128)S(1)}, u32[]{:S(2)}, u32[]{:S(2)}) collective-permute-start(f32[1,16,64,1]{3,1,2,0:T(8,128)S(1)} %get-tuple-element.55), channel_id=1, source_target_pairs={{1,0},{3,2},{5,4},{7,6},{9,8},{11,10},{13,12},{15,14},{17,16},{19,... | collective-permute-start | bytes 12296 | tf_op jit(solution)/shard_map/ppermute | solution.py:26
  108.1 5.9 %collective-permute-start.18 = (f32[1,1,64,128]{3,1,2,0:T(1,128)S(1)}, f32[1,1,64,128]{3,1,2,0:T(1,128)S(1)}, u32[]{:S(2)}, u32[]{:S(2)}) collective-permute-start(f32[1,1,64,128]{3,1,2,0:T(1,128)S(1)} %get-tuple-element.53), channel_id=1, source_target_pairs={{32,0},{64,32},{96,64},{128,96},{160,128},{192,160},{224,192},{256... | collective-permute-start | bytes 98312 | tf_op jit(solution)/shard_map/ppermute | solution.py:26
  109.4 5.6 %collective-permute-start.19 = (f32[1,1,64,128]{3,1,2,0:T(1,128)S(1)}, f32[1,1,64,128]{3,1,2,0:T(1,128)S(1)}, u32[]{:S(2)}, u32[]{:S(2)}) collective-permute-start(f32[1,1,64,128]{3,1,2,0:T(1,128)S(1)} %get-tuple-element.54), channel_id=1, source_target_pairs={{0,32},{32,64},{64,96},{96,128},{128,160},{160,192},{192,224},{224... | collective-permute-start | bytes 98312 | tf_op jit(solution)/shard_map/ppermute | solution.py:23
  115.2 5.8 %collective-permute-start.20 = (f32[1,16,1,128]{3,1,2,0:T(8,128)S(1)}, f32[1,16,1,128]{3,1,2,0:T(8,128)S(1)}, u32[]{:S(2)}, u32[]{:S(2)}) collective-permute-start(f32[1,16,1,128]{3,1,2,0:T(8,128)S(1)} %get-tuple-element.51), channel_id=1, source_target_pairs={{2,0},{4,2},{6,4},{8,6},{10,8},{12,10},{14,12},{16,14},{18,16},{20... | collective-permute-start | bytes 24584 | tf_op jit(solution)/shard_map/ppermute | solution.py:26
  116.5 5.3 %collective-permute-start.21 = (f32[1,16,1,128]{3,1,2,0:T(8,128)S(1)}, f32[1,16,1,128]{3,1,2,0:T(8,128)S(1)}, u32[]{:S(2)}, u32[]{:S(2)}) collective-permute-start(f32[1,16,1,128]{3,1,2,0:T(8,128)S(1)} %get-tuple-element.52), channel_id=1, source_target_pairs={{0,2},{2,4},{4,6},{6,8},{8,10},{10,12},{12,14},{14,16},{16,18},{18... | collective-permute-start | bytes 24584 | tf_op jit(solution)/shard_map/ppermute | solution.py:23
  122.2 5.3 %collective-permute-start.22 = (f32[1,16,64,1]{3,1,2,0:T(8,128)S(1)}, f32[1,16,64,1]{3,1,2,0:T(8,128)S(1)}, u32[]{:S(2)}, u32[]{:S(2)}) collective-permute-start(f32[1,16,64,1]{3,1,2,0:T(8,128)S(1)} %get-tuple-element.49), channel_id=1, source_target_pairs={{1,0},{3,2},{5,4},{7,6},{9,8},{11,10},{13,12},{15,14},{17,16},{19,... | collective-permute-start | bytes 12296 | tf_op jit(solution)/shard_map/ppermute | solution.py:26
  135.6 5.9 %collective-permute-start.24 = (f32[1,1,64,128]{3,1,2,0:T(1,128)S(1)}, f32[1,1,64,128]{3,1,2,0:T(1,128)S(1)}, u32[]{:S(2)}, u32[]{:S(2)}) collective-permute-start(f32[1,1,64,128]{3,1,2,0:T(1,128)S(1)} %get-tuple-element.47), channel_id=1, source_target_pairs={{32,0},{64,32},{96,64},{128,96},{160,128},{192,160},{224,192},{256... | collective-permute-start | bytes 98312 | tf_op jit(solution)/shard_map/ppermute | solution.py:26
  136.9 5.6 %collective-permute-start.25 = (f32[1,1,64,128]{3,1,2,0:T(1,128)S(1)}, f32[1,1,64,128]{3,1,2,0:T(1,128)S(1)}, u32[]{:S(2)}, u32[]{:S(2)}) collective-permute-start(f32[1,1,64,128]{3,1,2,0:T(1,128)S(1)} %get-tuple-element.48), channel_id=1, source_target_pairs={{0,32},{32,64},{64,96},{96,128},{128,160},{160,192},{192,224},{224... | collective-permute-start | bytes 98312 | tf_op jit(solution)/shard_map/ppermute | solution.py:23
  142.7 5.9 %collective-permute-start.26 = (f32[1,16,1,128]{3,1,2,0:T(8,128)S(1)}, f32[1,16,1,128]{3,1,2,0:T(8,128)S(1)}, u32[]{:S(2)}, u32[]{:S(2)}) collective-permute-start(f32[1,16,1,128]{3,1,2,0:T(8,128)S(1)} %get-tuple-element.45), channel_id=1, source_target_pairs={{2,0},{4,2},{6,4},{8,6},{10,8},{12,10},{14,12},{16,14},{18,16},{20... | collective-permute-start | bytes 24584 | tf_op jit(solution)/shard_map/ppermute | solution.py:26
  144.0 5.3 %collective-permute-start.27 = (f32[1,16,1,128]{3,1,2,0:T(8,128)S(1)}, f32[1,16,1,128]{3,1,2,0:T(8,128)S(1)}, u32[]{:S(2)}, u32[]{:S(2)}) collective-permute-start(f32[1,16,1,128]{3,1,2,0:T(8,128)S(1)} %get-tuple-element.46), channel_id=1, source_target_pairs={{0,2},{2,4},{4,6},{6,8},{8,10},{10,12},{12,14},{14,16},{16,18},{18... | collective-permute-start | bytes 24584 | tf_op jit(solution)/shard_map/ppermute | solution.py:23
  (16 other events, 52.5 us)
where the time goes:
time: 241 us; the launch traced here: 240 us
  starting transfers between devices  91.3 us (38%)
  blocking collectives  76.1 us (32%)
  local copies, waits for them, and re-layouts  20.3 us (8%)
  waiting for transfers between devices  17.4 us (7%)
  matrix products  16.2 us (7%)
  other arithmetic  12.6 us (5%)
  between operations  5.75 us (2%)
    psum x4, blocking collectives, by_axis(): return functools.reduce(lax.psum, axes, array)  76.1 us
    ppermute x15, starting transfers between devices, extended(): lax.ppermute(lax.slice_in_dim(block, block.shape[dim] - width, None, axis...  52.1 us
    ppermute x15, starting transfers between devices, extended(): lax.ppermute(lax.slice_in_dim(block, 0, width, axis=dim), axis, backward)  39.2 us
    ppermute x15, waiting for transfers between devices, extended(): lax.ppermute(lax.slice_in_dim(block, block.shape[dim] - width, None, axis...  17 us
    dot_general x4, matrix products, local_apply(): jnp.dot(block_x, field.reshape(size_x, -1), precision=high)  11 us
    slice x15, local copies, waits for them, and re-layouts, extended(): lax.slice_in_dim(block, 0, width, axis=dim)  5.16 us
  transfers between devices with their start and end apart: 30, of which 15 were waited for; matrix products, arithmetic and copies ran while one was open for 3% of the time, Pallas kernels for 0%

commit v1 on v0

v1 whole, which is shorter than its diff:
```python
import functools

import jax
import jax.numpy as jnp
import numpy as np
from jax import lax
from jax.experimental import pallas as pl
from jax.experimental.pallas import tpu as pltpu
from jax.sharding import PartitionSpec as P

MESH = pl.DeviceIdType.MESH
F32 = jnp.float32
BF16 = jnp.bfloat16
ROUNDS = 4

gll_inner = [0.20929921790247888, 0.5917001814331423, 0.8717401485096066]


def gll_tables():
    degree_val = 7
    points = np.array(
        [
            -1.0,
            -gll_inner[2],
            -gll_inner[1],
            -gll_inner[0],
            gll_inner[0],
            gll_inner[1],
            gll_inner[2],
            1.0,
        ]
    )
    previous = np.ones(8)
    values = points * 1.0
    for order in range(1, degree_val):
        following = ((2.0 * order + 1.0) * points * values - order * previous) / (order + 1.0)
        previous = values
        values = following
    weights = 2.0 / (degree_val * (degree_val + 1) * values**2)
    differ = points[:, None] - points[None, :]
    safe_gap = np.where(differ == 0.0, 1.0, differ)
    derivative = np.where(differ == 0.0, 0.0, values[:, None] / values[None, :] / safe_gap)
    corner_val = degree_val * (degree_val + 1) / 4.0
    ends_vec = np.concatenate([np.array([-corner_val]), np.zeros(6), np.array([corner_val])])
    index_row = np.arange(8)
    derivative = derivative + np.where(
        index_row[:, None] == index_row[None, :], ends_vec[None, :], 0.0
    )
    stiffness = derivative.T @ (weights[:, None] * derivative)
    return (weights, stiffness)


WEIGHTS, STIFF = gll_tables()
STIFF = 0.5 * (STIFF + STIFF[::-1, ::-1])
WEIGHTS = 0.5 * (WEIGHTS + WEIGHTS[::-1])


def halves(table):
    high = table.astype(np.float32).astype(jnp.dtype(BF16)).astype(np.float64)
    return high, table - high


def bf16_tables():
    scaled = STIFF / WEIGHTS[:, None]
    wide_z = np.kron(np.eye(16), scaled.T)
    high, low = halves(wide_z)
    along_z = np.block([[high, low], [high, np.zeros_like(low)]])
    wide_y = np.kron(np.eye(8), scaled)
    high, low = halves(wide_y)
    along_y = np.concatenate([high, high, low, np.zeros_like(low)], axis=1)
    return np.concatenate([along_z, along_y], axis=0).astype(np.float32)


def f32_tables():
    spread = np.kron(np.eye(16), np.ones((1, 8)))
    w, s = WEIGHTS, np.diagonal(STIFF)
    lanes = lambda v: np.tile(v, 16)[None, :]
    col = lambda v: v[:, None]
    parts = [spread, col(w) * lanes(w)]
    for p in range(8):
        diag = s[p] * col(w) * lanes(w) + w[p] * (col(s) * lanes(w) + col(w) * lanes(s))
        parts.append(1.0 / diag)
    return np.concatenate(parts, axis=0).astype(np.float32)


def smoother(
    nx,
    ny,
    f_ref,
    c_ref,
    lo_ref,
    up_ref,
    kb_ref,
    kf_ref,
    out_ref,
    ratio_ref,
    fb,
    xe0,
    yb0,
    y0,
    xy0,
    u,
    r,
    sol,
    inv,
    cb,
    wn,
    db,
    uz,
    yz,
    kb,
    kf,
    sx,
    rx,
    sy,
    ry,
    sd,
    rd,
    v1,
    a1,
    v2,
    a2,
    load_sem,
    send0,
    recv0,
    sends,
    recvs,
    out_send,
    out_recv,
    own_sem,
    s1_sem,
    r1_sem,
    s2_sem,
    r2_sem,
    far_y,
    far_x,
):
    gx = lax.axis_index("gx")
    gy = lax.axis_index("gy")
    t = lax.axis_index("gz")

    def at(dx, dy, core):
        return {"gx": lax.rem(gx + dx + nx, nx), "gy": lax.rem(gy + dy + ny, ny), "gz": core}

    def remote(src, dst, ss, rs, dev):
        return pltpu.make_async_remote_copy(
            src_ref=src, dst_ref=dst, send_sem=ss, recv_sem=rs, device_id=dev, device_id_type=MESH
        )

    barrier = pltpu.get_barrier_semaphore()
    count = 0
    for dx in (0, -1, 1):
        for dy in (0, -1, 1):
            for core in (1 - t, t):
                if dx == 0 and dy == 0 and core is t:
                    continue
                pl.semaphore_signal(
                    barrier, inc=1, device_id=at(dx, dy, core), device_id_type=MESH
                )
                count += 1

    loads = [
        pltpu.make_async_copy(f_ref, fb.at[t, :, pl.ds(0, 64)], load_sem.at[0]),
        pltpu.make_async_copy(kf_ref, kf, load_sem.at[1]),
        pltpu.make_async_copy(kb_ref, kb, load_sem.at[2]),
    ]
    for copy in loads:
        copy.start()

    row = lax.broadcasted_iota(jnp.int32, (8, 128), 0)
    lane = lax.broadcasted_iota(jnp.int32, (8, 128), 1)

    def z_sum(d0, d1):
        at_lane = lax.broadcasted_iota(jnp.int32, d0.shape, 1)
        k = lax.rem(at_lane, 8)
        ends = (k == 0) | (k == 7)
        up = k == 7
        axis = 1
        nxt0 = pltpu.roll(d0, 127, axis)
        nxt1 = pltpu.roll(d1, 127, axis)
        prv0 = pltpu.roll(d0, 1, axis)
        prv1 = pltpu.roll(d1, 1, axis)
        s0 = jnp.where(at_lane == 127, nxt1, jnp.where(up, nxt0, prv0))
        s1 = jnp.where(at_lane == 0, prv0, jnp.where(up, nxt1, prv1))
        zero = jnp.zeros_like(d0)
        return d0 + jnp.where(ends, s0, zero), d1 + jnp.where(ends, s1, zero)

    def spread_rows(value):
        return jnp.broadcast_to(value, (8, 128))

    loads[1].wait()
    ce = jnp.dot(
        c_ref[...].reshape(16, 16),
        kf[0:16, :],
        precision=lax.Precision.HIGHEST,
        preferred_element_type=F32,
    )
    for x, e in ((0, 0), (7, 0), (8, 1), (15, 1)):
        fb[t, x, 64:72, :] = ce[e * 8 : e * 8 + 8]
    loads[0].wait()
    for side, y in ((0, 0), (1, 63)):
        for b in range(2):
            for p in range(9):
                x = 15 - p if b else p
                yb0[side, b, p : p + 1, :] = fb[t, x, y : y + 1, :]
            e = 7 * side
            yb0[side, b, 9:10, :] = ce[b * 8 + e : b * 8 + e + 1]
            yb0[side, b, 10:11, :] = ce[(1 - b) * 8 + e : (1 - b) * 8 + e + 1]

    pl.semaphore_wait(barrier, count)

    mine = pl.ds(7 * (1 - t), 9)
    theirs = pl.ds(7 * t, 9)
    first = [
        remote(yb0.at[1, 1], xy0.at[0, t], send0.at[0], recv0.at[7 + t], at(1, 1, 0)),
        remote(yb0.at[0, 1], xy0.at[1, t], send0.at[1], recv0.at[9 + t], at(1, -1, 0)),
        remote(yb0.at[1, 0], xy0.at[0, t], send0.at[2], recv0.at[7 + t], at(-1, 1, 1)),
        remote(yb0.at[0, 0], xy0.at[1, t], send0.at[3], recv0.at[9 + t], at(-1, -1, 1)),
        remote(fb.at[t, 15], xe0.at[t], send0.at[4], recv0.at[1 + t], at(1, 0, 0)),
        remote(fb.at[t, 0], xe0.at[t], send0.at[5], recv0.at[1 + t], at(-1, 0, 1)),
        remote(fb.at[t, mine], fb.at[t, mine], send0.at[6], recv0.at[0], at(0, 0, 1 - t)),
        remote(yb0.at[1, 0], y0.at[0, t], send0.at[7], recv0.at[3 + t], at(0, 1, 0)),
        remote(yb0.at[1, 1], y0.at[0, t], send0.at[8], recv0.at[3 + t], at(0, 1, 1)),
        remote(yb0.at[0, 0], y0.at[1, t], send0.at[9], recv0.at[5 + t], at(0, -1, 0)),
        remote(yb0.at[0, 1], y0.at[1, t], send0.at[10], recv0.at[5 + t], at(0, -1, 1)),
    ]
    for copy in first:
        copy.start()

    def ring_signal(sem, axis, reach):
        for step in (reach, -reach):
            dev = at(step, 0, t) if axis == "gx" else at(0, step, t)
            pl.semaphore_signal(sem, inc=1, device_id=dev, device_id_type=MESH)

    hops_x = [h for h in (1, 2, 4, 8) if h < max(nx // 2, 1)]
    hops_y = [h for h in (1, 2, 4, 8) if h < max(ny // 2, 1)]

    def reach_step(i):
        if i > 0:
            if i - 1 < len(hops_x):
                pl.semaphore_wait(far_x.at[i - 1], 2)
            if i - 1 < len(hops_y):
                pl.semaphore_wait(far_y.at[i - 1], 2)
        if i < len(hops_x):
            ring_signal(far_x.at[i], "gx", hops_x[i])
        if i < len(hops_y):
            ring_signal(far_y.at[i], "gy", hops_y[i])

    reach_step(0)

    low = lo_ref[0]
    high = up_ref[0]
    centre = (high + low) / 2.0
    half = (high - low) / 2.0
    rho1 = half / centre
    rho2 = 1.0 / (2.0 * centre / half - rho1)
    first_scale = 1.0 / centre
    keep_scale = rho2 * rho1
    second_scale = 2.0 * rho2 / half

    last_y = ny * 64 - 1
    outer_x = jnp.where(t == 0, gx == 0, gx == nx - 1)
    inner_x = 1.0 - outer_x.astype(F32)
    z_half = jnp.where((lax.rem(lane, 8) == 0) | (lax.rem(lane, 8) == 7), 0.5, 1.0)
    yz_half = z_half * jnp.where((row == 0) | (row == 7), 0.5, 1.0)
    bound = {}
    for h in range(2):
        for e in range(8):
            keep = lane != (127 if h else 0)
            if e == 0:
                keep = keep & ((row + gy * 64) != 0)
            if e == 7:
                keep = keep & ((row + gy * 64 + 56) != last_y)
            bound[h, e] = jnp.where(keep, 1.0, 0.0)
            wn[h, e * 8 : e * 8 + 8, :] = bound[h, e] * yz_half

    def wait_for(dst, sem):
        remote(dst, dst, send0.at[0], sem, at(0, 0, 1 - t)).wait_recv()

    other = 1 - t
    wait_for(fb.at[other, theirs], recv0.at[0])
    for h in range(2):
        wait_for(xe0.at[h], recv0.at[1 + h])
        for side in range(2):
            wait_for(y0.at[side, h], recv0.at[3 + 2 * side + h])
            wait_for(xy0.at[side, h], recv0.at[7 + 2 * side + h])

    def plane(p):
        return p + t * (15 - 2 * p)

    def y_sum(rows_of):
        rows = [rows_of(0), rows_of(1)]
        for h in range(2):
            for p in range(8):
                a = db[h, p, pl.ds(7, 8, stride=8), :]
                b = db[h, p, pl.ds(0, 8, stride=8), :]
                from_high = spread_rows(rows[1][h][p : p + 1])
                from_low = spread_rows(rows[0][h][p : p + 1])
                up = jnp.where(row == 7, from_high, pltpu.roll(b, 7, 0))
                down = jnp.where(row == 0, from_low, pltpu.roll(a, 1, 0))
                db[h, p, pl.ds(7, 8, stride=8), :] = a + up
                db[h, p, pl.ds(0, 8, stride=8), :] = b + down

    for p in range(8):
        raw = []
        for h in range(2):
            d = fb[h, plane(p), 0:64, :]
            if p == 0:
                d = d + xe0[h, 0:64, :]
            if p == 7:
                d = d + fb[h, plane(8), 0:64, :]
            raw.append(d)
        db[0, p], db[1, p] = z_sum(*raw)

    def first_rows(side):
        raw = []
        for h in range(2):
            d = y0[side, h, 0:8, :]
            d = d + jnp.where(row == 0, spread_rows(xy0[side, h, 0:1, :]), 0.0)
            d = d + jnp.where(row == 7, spread_rows(y0[side, h, 8:9, :]), 0.0)
            raw.append(d)
        return z_sum(*raw)

    y_sum(first_rows)

    weight_jk = kf[16:24, :]
    for variant in range(3):
        own = [fb[h, plane(0), 64:72, :] for h in range(2)]
        near = [[spread_rows(y0[s, h, 9:10, :]) for h in range(2)] for s in range(2)]
        if variant == 0:
            for h in range(2):
                for e in range(8):
                    cb[h, e * 8 : e * 8 + 8, :] = spread_rows(own[h][e : e + 1]) * weight_jk
        if variant == 1:
            own = [own[h] + xe0[h, 64:72, :] for h in range(2)]
            near = [
                [near[s][h] + spread_rows(xy0[s, h, 9:10, :]) for h in range(2)] for s in range(2)
            ]
        if variant == 2:
            own = [own[h] + fb[h, plane(8), 64:72, :] for h in range(2)]
            near = [
                [near[s][h] + spread_rows(y0[s, h, 10:11, :]) for h in range(2)] for s in range(2)
            ]
        own = z_sum(*own)
        near = [z_sum(*pair) for pair in near]
        for h in range(2):
            a = own[h] + jnp.where(row == 7, near[1][h], pltpu.roll(own[h], 7, 0))
            b = own[h] + jnp.where(row == 0, near[0][h], pltpu.roll(own[h], 1, 0))
            for e in range(8):
                one = slice(e, e + 1)
                tile = jnp.where(
                    row == 7,
                    spread_rows(a[one]),
                    jnp.where(row == 0, spread_rows(b[one]), spread_rows(own[h][one])),
                )
                flip = bound[h, e] / tile
                if variant == 1:
                    flip = flip * inner_x
                for p in {0: range(1, 7), 1: (0,), 2: (7,)}[variant]:
                    inv[h, p, e * 8 : e * 8 + 8, :] = flip * kf[24 + 8 * p : 32 + 8 * p, :]

    reach_step(1)
    loads[2].wait()

    stiff = STIFF
    even = [[float(stiff[p, i] + stiff[p, 7 - i]) / 2 for i in range(4)] for p in range(4)]
    odd = [[float(stiff[p, i] - stiff[p, 7 - i]) / 2 for i in range(4)] for p in range(4)]

    def norm_of(acc):
        return jnp.sum(acc)

    def update(step):
        total = jnp.zeros((8, 128), F32)
        for h in range(2):
            for p in range(8):
                if step == 0:
                    res = db[h, p]
                else:
                    res = r[h, p] - db[h, p]
                if step % 2 == 0:
                    square = res * res * wn[h]
                    part = jnp.sum(square.reshape(8, 8, 128), axis=0)
                    if p == 0:
                        part = part * (0.5 * inner_x)
                    if p == 7:
                        part = part * 0.5
                    total = total + part
                if step == ROUNDS:
                    continue
                r[h, p] = res
                if step % 2 == 0:
                    new = inv[h, p] * (res * first_scale)
                else:
                    new = keep_scale * u[h, p] + second_scale * (inv[h, p] * res)
                u[h, p] = new
                home = p + t * (7 - 2 * p)
                sol[h, home] = new if step == 0 else sol[h, home] + new
                top = new.astype(BF16)
                uz[h, p, :, 0:128] = top
                uz[h, p, :, 128:256] = (new - top.astype(F32)).astype(BF16)
        return total

    def apply(k):
        along_z = kb[0:256, :]
        for h in range(2):
            out = jnp.dot(uz[h].reshape(512, 256), along_z, preferred_element_type=F32)
            yz[h] = (out[:, 0:128] + out[:, 128:256]).reshape(8, 64, 128)
        along_y = kb[256:320, 0:192]
        for p in range(8):
            top = jnp.concatenate([uz[0, p, :, 0:128], uz[1, p, :, 0:128]], axis=1)
            low_part = jnp.concatenate([uz[0, p, :, 128:256], uz[1, p, :, 128:256]], axis=1)
            both = jnp.concatenate([top, low_part, top], axis=0)
            out = jnp.dot(along_y, both, preferred_element_type=F32)
            for h in range(2):
                yz[h, p] = yz[h, p] + out[:, h * 128 : h * 128 + 128]
        for h in range(2):
            for e in range(8):
                rows = pl.ds(e * 8, 8)
                val = [u[h, p, rows, :] for p in range(8)]
                plus = [(val[i] + val[7 - i]) for i in range(4)]
                minus = [(val[i] - val[7 - i]) for i in range(4)]
                coef = cb[h, rows, :]
                for p in range(4):
                    ev = sum(even[p][i] * plus[i] for i in range(4))
                    od = sum(odd[p][i] * minus[i] for i in range(4))
                    w = float(WEIGHTS[p])
                    d_low = coef * (ev + od + w * yz[h, p, rows, :])
                    d_high = coef * (ev - od + w * yz[h, 7 - p, rows, :])
                    db[h, p, rows, :] = d_low
                    db[h, 7 - p, rows, :] = d_high
                    if p == 0:
                        sx[k, 0, h, rows, :] = d_low
                        sx[k, 1, h, rows, :] = d_high
                    if e in (0, 7):
                        side = 0 if e == 0 else 1
                        j = 0 if e == 0 else 7
                        sy[k, side, h, p : p + 1, :] = d_low[j : j + 1]
                        sy[k, side, h, 7 - p : 8 - p, :] = d_high[j : j + 1]
                        if p == 0:
                            sd[k, 0, side, h : h + 1, :] = d_low[j : j + 1]
                            sd[k, 1, side, h : h + 1, :] = d_high[j : j + 1]

    def messages(k):
        ss = sends.at[k]
        rs = recvs.at[k]
        ext = 2 * t - 1
        return [
            remote(sd.at[k, 0, 0], rd.at[k, 0, 1], ss.at[4], rs.at[5], at(ext, -1, other)),
            remote(sd.at[k, 0, 1], rd.at[k, 0, 0], ss.at[5], rs.at[4], at(ext, 1, other)),
            remote(sx.at[k, 0], rx.at[k, 0], ss.at[0], rs.at[0], at(ext, 0, other)),
            remote(sd.at[k, 1, 0], rd.at[k, 1, 1], ss.at[6], rs.at[7], at(0, -1, other)),
            remote(sd.at[k, 1, 1], rd.at[k, 1, 0], ss.at[7], rs.at[6], at(0, 1, other)),
            remote(sy.at[k, 0], ry.at[k, 1], ss.at[2], rs.at[3], at(0, -1, t)),
            remote(sy.at[k, 1], ry.at[k, 0], ss.at[3], rs.at[2], at(0, 1, t)),
            remote(sx.at[k, 1], rx.at[k, 1], ss.at[1], rs.at[1], at(0, 0, other)),
        ]

    def assemble(k):
        copies = messages(k)
        for copy in copies:
            copy.start()
        for p in range(1, 7):
            db[0, p], db[1, p] = z_sum(db[0, p], db[1, p])
        for copy in copies:
            copy.wait_recv()
        for side, p in ((0, 0), (1, 7)):
            db[0, p], db[1, p] = z_sum(
                db[0, p] + rx[k, side, 0], db[1, p] + rx[k, side, 1]
            )

        def rows_of(side):
            raw = []
            for h in range(2):
                d = ry[k, side, h]
                d = d + jnp.where(row == 0, spread_rows(rd[k, 0, side, h : h + 1, :]), 0.0)
                d = d + jnp.where(row == 7, spread_rows(rd[k, 1, side, h : h + 1, :]), 0.0)
                raw.append(d)
            return z_sum(*raw)

        y_sum(rows_of)
        return copies

    sent = list(first)
    norms = []
    tail = []
    for step in range(ROUNDS):
        total = update(step)
        if step % 2 == 0:
            norms.append(norm_of(total))
        if step == ROUNDS - 1:
            half_rows = pl.ds(8 * t, 8)
            away = remote(
                sol.at[other], out_ref.at[half_rows], out_send, out_recv, at(0, 0, other)
            )
            home = pltpu.make_async_copy(sol.at[t], out_ref.at[half_rows], own_sem)
            away.start()
            home.start()
            tail = [away, home]
        apply(step)
        sent += assemble(step)
        reach_step(step + 2)
    norms.append(norm_of(update(ROUNDS)))

    lane1 = lax.broadcasted_iota(jnp.int32, (1, 128), 1)
    line = jnp.where(lane1 == 0, norms[0], jnp.where(lane1 == 1, norms[1], norms[2]))
    v1[...] = line
    hops = []
    for o in range(1, ny):
        hops.append(remote(v1, a1.at[gy], s1_sem.at[o], r1_sem.at[gy], at(0, o, t)))
    for copy in hops:
        copy.start()
    a1[gy] = line
    for o in range(1, ny):
        source = lax.rem(gy + o, ny)
        wait_for(a1.at[source], r1_sem.at[source])
    line = jnp.sum(a1[...], axis=0)
    v2[...] = line
    slot = gx * 2 + t
    wide = []
    for o in range(0, nx):
        for flip in range(2):
            if o == 0 and flip == 0:
                continue
            core = other if flip else t
            i = 2 * o + flip
            wide.append(remote(v2, a2.at[slot], s2_sem.at[i], r2_sem.at[slot], at(o, 0, core)))
    for copy in wide:
        copy.start()
    a2[slot] = line
    for o in range(0, nx):
        for flip in range(2):
            if o == 0 and flip == 0:
                continue
            source = lax.rem(gx + o, nx) * 2 + (other if flip else t)
            wait_for(a2.at[source], r2_sem.at[source])
    line = jnp.sum(a2[...], axis=0)
    whole = line[0, 0]
    ratio_ref[...] = jnp.sqrt(line / whole)

    tail[0].wait_recv()
    tail[1].wait()
    for copy in sent + hops + wide + tail[:1]:
        copy.wait_send()


def per_device(nx, ny, forcing, conductivity, lower_bound, upper_bound):
    vmem = lambda *shape: pltpu.VMEM(shape, F32)
    dma = lambda *shape: pltpu.SemaphoreType.DMA(shape)
    scratch = [
        vmem(2, 16, 72, 128),
        vmem(2, 72, 128),
        vmem(2, 2, 16, 128),
        vmem(2, 2, 16, 128),
        vmem(2, 2, 16, 128),
        vmem(2, 8, 64, 128),
        vmem(2, 8, 64, 128),
        vmem(2, 8, 64, 128),
        vmem(2, 8, 64, 128),
        vmem(2, 64, 128),
        vmem(2, 64, 128),
        vmem(2, 8, 64, 128),
        pltpu.VMEM((2, 8, 64, 256), BF16),
        vmem(2, 8, 64, 128),
        pltpu.VMEM((320, 256), BF16),
        vmem(88, 128),
        vmem(ROUNDS, 2, 2, 64, 128),
        vmem(ROUNDS, 2, 2, 64, 128),
        vmem(ROUNDS, 2, 2, 8, 128),
        vmem(ROUNDS, 2, 2, 8, 128),
        vmem(ROUNDS, 2, 2, 2, 128),
        vmem(ROUNDS, 2, 2, 2, 128),
        vmem(1, 128),
        vmem(ny, 1, 128),
        vmem(1, 128),
        vmem(2 * nx, 1, 128),
        dma(3),
        dma(11),
        dma(11),
        dma(ROUNDS, 8),
        dma(ROUNDS, 8),
        dma(),
        dma(),
        dma(),
        dma(ny),
        dma(ny),
        dma(2 * nx),
        dma(2 * nx),
        pltpu.SemaphoreType.REGULAR((4,)),
        pltpu.SemaphoreType.REGULAR((4,)),
    ]
    anywhere = pl.BlockSpec(memory_space=pl.ANY)
    in_vmem = pl.BlockSpec(memory_space=pltpu.VMEM)
    in_smem = pl.BlockSpec(memory_space=pltpu.SMEM)
    result, line = pl.pallas_call(
        functools.partial(smoother, nx, ny),
        out_shape=(
            jax.ShapeDtypeStruct(forcing.shape, F32),
            jax.ShapeDtypeStruct((1, 128), F32),
        ),
        in_specs=[anywhere, in_vmem, in_smem, in_smem, anywhere, anywhere],
        out_specs=(anywhere, in_vmem),
        scratch_shapes=scratch,
        compiler_params=pltpu.CompilerParams(collective_id=0, has_side_effects=True),
    )(
        forcing,
        conductivity,
        lower_bound,
        upper_bound,
        jnp.asarray(bf16_tables(), BF16),
        jnp.asarray(f32_tables(), F32),
    )
    return result, line[0, 1:3]


def solution(mesh):
    spec = P("gx", "gy", "gz")
    return jax.shard_map(
        functools.partial(per_device, mesh.shape["gx"], mesh.shape["gy"]),
        mesh=mesh,
        in_specs=(spec, spec, P(), P()),
        out_specs=(spec, P()),
        check_vma=False,
    )
```

time: 241 us -> 63.2 us (0.26)
  starting transfers between devices: 91.3 us -> 0 us
  blocking collectives: 76.1 us -> 0 us
  Pallas kernels: 0 us -> 57.8 us
  waiting for transfers between devices: 17.4 us -> 0 us
  local copies, waits for them, and re-layouts: 20.3 us -> 3.13 us
  matrix products: 16.2 us -> 0 us
  other arithmetic: 12.6 us -> 0 us
  between operations: 5.75 us -> 1.94 us
    ppermute x30 -> x0, starting transfers between devices: 91.3 us -> none  [the longest x15 52.1 us: extended(): lax.ppermute(lax.slice_in_dim(block, block.shape[dim] - width, None, axis...]
    psum x4 -> x0, blocking collectives: 76.1 us -> none  [by_axis(): return functools.reduce(lax.psum, axes, array)]
    pallas_call x0 -> x1, Pallas kernels: none -> 57.8 us  [per_device(): pl.pallas_call(functools.partial(smoother, nx, ny), out_shape=(jax.ShapeD...]
    ppermute x30 -> x0, waiting for transfers between devices: 17.4 us -> none  [the longest x15 17 us: extended(): lax.ppermute(lax.slice_in_dim(block, block.shape[dim] - width, None, axis...]
    dot_general x12 -> x0, matrix products: 16.2 us -> none  [the longest x4 11 us: local_apply(): jnp.dot(block_x, field.reshape(size_x, -1), precision=high)]
    add x17 -> x0, other arithmetic: 7.71 us -> none  [the longest x11 4.73 us: pair_sum(): centre + jnp.reshape(is_last, view_shape) * upper_side]
    slice x18 -> x0, local copies, waits for them, and re-layouts: 7.16 us -> none  [the longest x15 5.16 us: extended(): lax.slice_in_dim(block, 0, width, axis=dim)]
    ppermute x2 -> x0, local copies, waits for them, and re-layouts: 2.9 us -> none  [the longest x1 1.45 us: extended(): lax.ppermute(lax.slice_in_dim(block, 0, width, axis=dim), axis, backward)]
  transfers between devices with their start and end apart: 30 -> 0, of which waited for: 15 -> 0; matrix products, arithmetic and copies ran while one was open for 3% -> 0% of each run, Pallas kernels for 0% -> 0%
where the time goes in v1:
time: 63.2 us; the launch traced here: 62.9 us
  Pallas kernels  57.8 us (91%)
  local copies, waits for them, and re-layouts  3.13 us (5%)
  between operations  1.94 us (3%)
    pallas_call x1, Pallas kernels, per_device(): pl.pallas_call(functools.partial(smoother, nx, ny), out_shape=(jax.ShapeD...  57.8 us
    unnamed x3, local copies, waits for them, and re-layouts  2.55 us

profile of v1, /device:TPU:1, one launch (start us, length us, event | category | flops | bytes accessed | tf_op | source)
XLA Modules:
  0.0 62.9 jit_solution(13127640293292182605)
XLA Ops:
  1.9 57.8 %shard_map.77 = (f32[16,64,128]{2,1,0:T(8,128)}, f32[1,128]{1,0:T(1,128)}) custom-call(f32[16,64,128]{2,1,0:T(8,128)} %f_ref.1, f32[2,8,16]{2,1,0:T(8,128)} %c_ref.1, f32[1]{0:T(128)S(6)} %copy.9.lo_ref, f32[1]{0:T(128)S(6)} %copy.10.up_ref, bf16[320,256]{1,0:T(8,128)(2,1)} %constant.4.clone.kb_ref, f32[88,128]{1,0:T(8,128)} %constant.5.clone.kf_ref), custom_call_target="tpu_custom_call" | custom-call | tf_op jit(solution)/shard_map/pallas_call | solution.py:594
  59.8 0.0 copy-start
  59.8 0.7 %copy-done = f32[1,128]{1,0:T(1,128)S(1)} copy-done((f32[1,128]{1,0:T(1,128)S(1)}, f32[1,128]{1,0:T(1,128)}, u32[]{:S(2)}) %copy-start) | copy-done | bytes 536
  60.4 0.6 slice_bitcast_fusion
  61.0 1.9 %copy.11 = f32[16,64,128]{2,1,0:T(8,128)} copy(f32[16,64,128]{2,1,0:T(8,128)} %get-tuple-element.8) | data formatting | bytes 1048576
Async XLA Ops:
  59.8 0.7 %copy-start = (f32[1,128]{1,0:T(1,128)S(1)}, f32[1,128]{1,0:T(1,128)}, u32[]{:S(2)}) copy-start(f32[1,128]{1,0:T(1,128)} %get-tuple-element.5) | copy-start | bytes 1540

commit v2 on v1

--- a/solution.py
+++ b/solution.py
@@ -120,6 +120,9 @@
     a1,
     v2,
     a2,
+    cv,
+    lo_s,
+    up_s,
     load_sem,
     send0,
     recv0,
@@ -127,7 +130,6 @@
     recvs,
     out_send,
     out_recv,
-    own_sem,
     s1_sem,
     r1_sem,
     s2_sem,
@@ -149,8 +151,8 @@
 
     barrier = pltpu.get_barrier_semaphore()
     count = 0
-    for dx in (0, -1, 1):
-        for dy in (0, -1, 1):
+    for dx in (-1, 1, 0):
+        for dy in (-1, 1, 0):
             for core in (1 - t, t):
                 if dx == 0 and dy == 0 and core is t:
                     continue
@@ -163,6 +165,9 @@
         pltpu.make_async_copy(f_ref, fb.at[t, :, pl.ds(0, 64)], load_sem.at[0]),
         pltpu.make_async_copy(kf_ref, kf, load_sem.at[1]),
         pltpu.make_async_copy(kb_ref, kb, load_sem.at[2]),
+        pltpu.make_async_copy(c_ref, cv, load_sem.at[3]),
+        pltpu.make_async_copy(lo_ref, lo_s, load_sem.at[4]),
+        pltpu.make_async_copy(up_ref, up_s, load_sem.at[5]),
     ]
     for copy in loads:
         copy.start()
@@ -189,8 +194,9 @@
         return jnp.broadcast_to(value, (8, 128))
 
     loads[1].wait()
+    loads[3].wait()
     ce = jnp.dot(
-        c_ref[...].reshape(16, 16),
+        cv[...].reshape(16, 16),
         kf[0:16, :],
         precision=lax.Precision.HIGHEST,
         preferred_element_type=F32,
@@ -248,8 +254,10 @@
 
     reach_step(0)
 
-    low = lo_ref[0]
-    high = up_ref[0]
+    loads[4].wait()
+    loads[5].wait()
+    low = lo_s[0]
+    high = up_s[0]
     centre = (high + low) / 2.0
     half = (high - low) / 2.0
     rho1 = half / centre
@@ -277,40 +285,51 @@
     def wait_for(dst, sem):
         remote(dst, dst, send0.at[0], sem, at(0, 0, 1 - t)).wait_recv()
 
+    def plane(p):
+        return p + t * (15 - 2 * p)
+
+    def y_own(planes):
+        for h in range(2):
+            for p in planes:
+                a = db[h, p, pl.ds(7, 8, stride=8), :]
+                b = db[h, p, pl.ds(0, 8, stride=8), :]
+                db[h, p, pl.ds(7, 8, stride=8), :] = a + jnp.where(
+                    row == 7, 0.0, pltpu.roll(b, 7, 0)
+                )
+                db[h, p, pl.ds(0, 8, stride=8), :] = b + jnp.where(
+                    row == 0, 0.0, pltpu.roll(a, 1, 0)
+                )
+
+    def y_add(rows_of):
+        low_rows, high_rows = rows_of(0), rows_of(1)
+        for h in range(2):
+            for p in range(8):
+                one = slice(p, p + 1)
+                db[h, p, 0:1, :] = db[h, p, 0:1, :] + low_rows[h][one]
+                db[h, p, 63:64, :] = db[h, p, 63:64, :] + high_rows[h][one]
+
     other = 1 - t
+    weight_jk = kf[16:24, :]
     wait_for(fb.at[other, theirs], recv0.at[0])
+    own_c = [fb[h, plane(0), 64:72, :] for h in range(2)]
+    int_c = [fb[h, plane(8), 64:72, :] for h in range(2)]
+    for h in range(2):
+        for e in range(8):
+            cb[h, e * 8 : e * 8 + 8, :] = spread_rows(own_c[h][e : e + 1]) * weight_jk
+    for p in range(1, 7):
+        db[0, p], db[1, p] = z_sum(fb[0, plane(p), 0:64, :], fb[1, plane(p), 0:64, :])
+    y_own(range(1, 7))
+    db[0, 7], db[1, 7] = z_sum(
+        *[fb[h, plane(7), 0:64, :] + fb[h, plane(8), 0:64, :] for h in range(2)]
+    )
     for h in range(2):
         wait_for(xe0.at[h], recv0.at[1 + h])
         for side in range(2):
             wait_for(y0.at[side, h], recv0.at[3 + 2 * side + h])
             wait_for(xy0.at[side, h], recv0.at[7 + 2 * side + h])
-
-    def plane(p):
-        return p + t * (15 - 2 * p)
-
-    def y_sum(rows_of):
-        rows = [rows_of(0), rows_of(1)]
-        for h in range(2):
-            for p in range(8):
-                a = db[h, p, pl.ds(7, 8, stride=8), :]
-                b = db[h, p, pl.ds(0, 8, stride=8), :]
-                from_high = spread_rows(rows[1][h][p : p + 1])
-                from_low = spread_rows(rows[0][h][p : p + 1])
-                up = jnp.where(row == 7, from_high, pltpu.roll(b, 7, 0))
-                down = jnp.where(row == 0, from_low, pltpu.roll(a, 1, 0))
-                db[h, p, pl.ds(7, 8, stride=8), :] = a + up
-                db[h, p, pl.ds(0, 8, stride=8), :] = b + down
-
-    for p in range(8):
-        raw = []
-        for h in range(2):
-            d = fb[h, plane(p), 0:64, :]
-            if p == 0:
-                d = d + xe0[h, 0:64, :]
-            if p == 7:
-                d = d + fb[h, plane(8), 0:64, :]
-            raw.append(d)
-        db[0, p], db[1, p] = z_sum(*raw)
+    db[0, 0], db[1, 0] = z_sum(
+        *[fb[h, plane(0), 0:64, :] + xe0[h, 0:64, :] for h in range(2)]
+    )
 
     def first_rows(side):
         raw = []
@@ -321,23 +340,19 @@
             raw.append(d)
         return z_sum(*raw)
 
-    y_sum(first_rows)
-
-    weight_jk = kf[16:24, :]
+    y_own((0, 7))
+    y_add(first_rows)
+
     for variant in range(3):
-        own = [fb[h, plane(0), 64:72, :] for h in range(2)]
+        own = own_c
         near = [[spread_rows(y0[s, h, 9:10, :]) for h in range(2)] for s in range(2)]
-        if variant == 0:
-            for h in range(2):
-                for e in range(8):
-                    cb[h, e * 8 : e * 8 + 8, :] = spread_rows(own[h][e : e + 1]) * weight_jk
         if variant == 1:
             own = [own[h] + xe0[h, 64:72, :] for h in range(2)]
             near = [
                 [near[s][h] + spread_rows(xy0[s, h, 9:10, :]) for h in range(2)] for s in range(2)
             ]
         if variant == 2:
-            own = [own[h] + fb[h, plane(8), 64:72, :] for h in range(2)]
+            own = [own[h] + int_c[h] for h in range(2)]
             near = [
                 [near[s][h] + spread_rows(y0[s, h, 10:11, :]) for h in range(2)] for s in range(2)
             ]
@@ -461,6 +476,10 @@
             copy.start()
         for p in range(1, 7):
             db[0, p], db[1, p] = z_sum(db[0, p], db[1, p])
+        y_own(range(1, 7))
+        if k == ROUNDS - 1:
+            for p in range(8):
+                out_ref[8 * t + p] = sol[t, p]
         for copy in copies:
             copy.wait_recv()
         for side, p in ((0, 0), (1, 7)):
@@ -477,7 +496,8 @@
                 raw.append(d)
             return z_sum(*raw)
 
-        y_sum(rows_of)
+        y_own((0, 7))
+        y_add(rows_of)
         return copies
 
     sent = list(first)
@@ -492,10 +512,8 @@
             away = remote(
                 sol.at[other], out_ref.at[half_rows], out_send, out_recv, at(0, 0, other)
             )
-            home = pltpu.make_async_copy(sol.at[t], out_ref.at[half_rows], own_sem)
             away.start()
-            home.start()
-            tail = [away, home]
+            tail = [away]
         apply(step)
         sent += assemble(step)
         reach_step(step + 2)
@@ -535,10 +553,9 @@
             wait_for(a2.at[source], r2_sem.at[source])
     line = jnp.sum(a2[...], axis=0)
     whole = line[0, 0]
-    ratio_ref[...] = jnp.sqrt(line / whole)
+    ratio_ref[...] = pltpu.roll(jnp.sqrt(line / whole), 127, 1)[:, 0:2]
 
     tail[0].wait_recv()
-    tail[1].wait()
     for copy in sent + hops + wide + tail[:1]:
         copy.wait_send()
 
@@ -573,12 +590,14 @@
         vmem(ny, 1, 128),
         vmem(1, 128),
         vmem(2 * nx, 1, 128),
-        dma(3),
+        vmem(2, 8, 16),
+        pltpu.SMEM((1,), F32),
+        pltpu.SMEM((1,), F32),
+        dma(6),
         dma(11),
         dma(11),
         dma(ROUNDS, 8),
         dma(ROUNDS, 8),
-        dma(),
         dma(),
         dma(),
         dma(ny),
@@ -590,15 +609,14 @@
     ]
     anywhere = pl.BlockSpec(memory_space=pl.ANY)
     in_vmem = pl.BlockSpec(memory_space=pltpu.VMEM)
-    in_smem = pl.BlockSpec(memory_space=pltpu.SMEM)
     result, line = pl.pallas_call(
         functools.partial(smoother, nx, ny),
         out_shape=(
-            jax.ShapeDtypeStruct(forcing.shape, F32),
-            jax.ShapeDtypeStruct((1, 128), F32),
+            pltpu.VMEM(forcing.shape, F32),
+            jax.ShapeDtypeStruct((1, 2), F32),
         ),
-        in_specs=[anywhere, in_vmem, in_smem, in_smem, anywhere, anywhere],
-        out_specs=(anywhere, in_vmem),
+        in_specs=[anywhere] * 6,
+        out_specs=(in_vmem, in_vmem),
         scratch_shapes=scratch,
         compiler_params=pltpu.CompilerParams(collective_id=0, has_side_effects=True),
     )(
@@ -609,7 +627,7 @@
         jnp.asarray(bf16_tables(), BF16),
         jnp.asarray(f32_tables(), F32),
     )
-    return result, line[0, 1:3]
+    return result, line.reshape(2)
 
 
 def solution(mesh):

time: 63.2 us -> 60.9 us (0.964)
  local copies, waits for them, and re-layouts: 3.13 us -> 1.93 us
  Pallas kernels: 57.8 us -> 56.9 us
    pallas_call x1, Pallas kernels: 57.8 us -> 56.9 us  [per_device(): pl.pallas_call(functools.partial(smoother, nx, ny), out_shape=(pltpu.VMEM...]
    unnamed x3 -> x4, local copies, waits for them, and re-layouts: 2.55 us -> 1.93 us
where the time goes in v2:
time: 60.9 us; the launch traced here: 60.8 us
  Pallas kernels  56.9 us (93%)
  local copies, waits for them, and re-layouts  1.93 us (3%)
  between operations  1.93 us (3%)
    pallas_call x1, Pallas kernels, per_device(): pl.pallas_call(functools.partial(smoother, nx, ny), out_shape=(pltpu.VMEM...  56.9 us
    unnamed x4, local copies, waits for them, and re-layouts  1.93 us

profile of v2, /device:TPU:1, one launch (start us, length us, event | category | flops | bytes accessed | tf_op | source)
XLA Modules:
  0.0 60.8 jit_solution(5083399551537061658)
XLA Ops:
  1.9 56.9 %shard_map.77 = (f32[16,64,128]{2,1,0:T(8,128)S(1)}, f32[1,2]{1,0:T(1,128)}) custom-call(f32[16,64,128]{2,1,0:T(8,128)} %f_ref.1, f32[2,8,16]{2,1,0:T(8,128)} %c_ref.1, f32[1]{0:T(128)S(6)} %copy.11.lo_ref, f32[1]{0:T(128)S(6)} %copy.12.up_ref, bf16[320,256]{1,0:T(8,128)(2,1)} %constant.4.clone.kb_ref, f32[88,128]{1,0:T(8,128)} %constant.5.clone.kf_ref), custom_call_target="tpu_custom_call" | custom-call | tf_op jit(solution)/shard_map/pallas_call | solution.py:612
  58.8 0.8 %copy.10 = f32[16,64,128]{2,1,0:T(8,128)} copy(f32[16,64,128]{2,1,0:T(8,128)S(1)} %get-tuple-element.6) | data formatting | bytes 1048576
  59.6 0.0 copy-start
  59.6 0.6 %copy-done = f32[1,2]{1,0:T(1,128)S(1)} copy-done((f32[1,2]{1,0:T(1,128)S(1)}, f32[1,2]{1,0:T(1,128)}, u32[]{:S(2)}) %copy-start) | copy-done | bytes 32
  60.2 0.5 copy.13
Async XLA Ops:
  59.6 0.6 %copy-start = (f32[1,2]{1,0:T(1,128)S(1)}, f32[1,2]{1,0:T(1,128)}, u32[]{:S(2)}) copy-start(f32[1,2]{1,0:T(1,128)} %get-tuple-element.5) | copy-start | bytes 28

commit v3 on v2

--- a/solution.py
+++ b/solution.py
@@ -68,7 +68,9 @@
     wide_y = np.kron(np.eye(8), scaled)
     high, low = halves(wide_y)
     along_y = np.concatenate([high, high, low, np.zeros_like(low)], axis=1)
-    return np.concatenate([along_z, along_y], axis=0).astype(np.float32)
+    few_high, few_low = high[:32, :32], low[:32, :32]
+    few = np.concatenate([few_high, few_high, few_low, np.zeros((32, 160))], axis=1)
+    return np.concatenate([along_z, along_y, few], axis=0).astype(np.float32)
 
 
 def f32_tables():
@@ -384,17 +386,23 @@
     def norm_of(acc):
         return jnp.sum(acc)
 
-    def update(step):
+    regions = {
+        "inner": [(p, 16, 32) for p in range(1, 7)],
+        "outer": [(0, 0, 64), (7, 0, 64)]
+        + [(p, first, 16) for p in range(1, 7) for first in (0, 48)],
+    }
+
+    def update(step, region):
         total = jnp.zeros((8, 128), F32)
         for h in range(2):
-            for p in range(8):
-                if step == 0:
-                    res = db[h, p]
-                else:
-                    res = r[h, p] - db[h, p]
+            for p, first_row, n in regions[region]:
+                rows = pl.ds(first_row, n)
+                res = db[h, p, rows, :]
+                if step > 0:
+                    res = r[h, p, rows, :] - res
                 if step % 2 == 0:
-                    square = res * res * wn[h]
-                    part = jnp.sum(square.reshape(8, 8, 128), axis=0)
+                    square = res * res * wn[h, rows, :]
+                    part = jnp.sum(square.reshape(n // 8, 8, 128), axis=0)
                     if p == 0:
                         part = part * (0.5 * inner_x)
                     if p == 7:
@@ -402,58 +410,83 @@
                     total = total + part
                 if step == ROUNDS:
                     continue
-                r[h, p] = res
+                r[h, p, rows, :] = res
                 if step % 2 == 0:
-                    new = inv[h, p] * (res * first_scale)
+                    new = inv[h, p, rows, :] * (res * first_scale)
                 else:
-                    new = keep_scale * u[h, p] + second_scale * (inv[h, p] * res)
-                u[h, p] = new
+                    new = keep_scale * u[h, p, rows, :] + second_scale * (inv[h, p, rows, :] * res)
+                u[h, p, rows, :] = new
                 home = p + t * (7 - 2 * p)
-                sol[h, home] = new if step == 0 else sol[h, home] + new
+                sol[h, home, rows, :] = new if step == 0 else sol[h, home, rows, :] + new
                 top = new.astype(BF16)
-                uz[h, p, :, 0:128] = top
-                uz[h, p, :, 128:256] = (new - top.astype(F32)).astype(BF16)
+                uz[h, p, rows, 0:128] = top
+                uz[h, p, rows, 128:256] = (new - top.astype(F32)).astype(BF16)
         return total
 
-    def apply(k):
+    def multiply(region):
         along_z = kb[0:256, :]
-        for h in range(2):
-            out = jnp.dot(uz[h].reshape(512, 256), along_z, preferred_element_type=F32)
-            yz[h] = (out[:, 0:128] + out[:, 128:256]).reshape(8, 64, 128)
-        along_y = kb[256:320, 0:192]
+        many = kb[256:320, 0:192]
+        few = kb[320:352, 0:96]
+        parts = regions[region]
+        for h in range(2):
+            lhs = jnp.concatenate([uz[h, p, pl.ds(f, n), :] for p, f, n in parts], axis=0)
+            out = jnp.dot(lhs, along_z, preferred_element_type=F32)
+            out = out[:, 0:128] + out[:, 128:256]
+            at_row = 0
+            for p, f, n in parts:
+                yz[h, p, pl.ds(f, n), :] = out[at_row : at_row + n]
+                at_row += n
         for p in range(8):
-            top = jnp.concatenate([uz[0, p, :, 0:128], uz[1, p, :, 0:128]], axis=1)
-            low_part = jnp.concatenate([uz[0, p, :, 128:256], uz[1, p, :, 128:256]], axis=1)
-            both = jnp.concatenate([top, low_part, top], axis=0)
-            out = jnp.dot(along_y, both, preferred_element_type=F32)
-            for h in range(2):
-                yz[h, p] = yz[h, p] + out[:, h * 128 : h * 128 + 128]
-        for h in range(2):
-            for e in range(8):
-                rows = pl.ds(e * 8, 8)
-                val = [u[h, p, rows, :] for p in range(8)]
-                plus = [(val[i] + val[7 - i]) for i in range(4)]
-                minus = [(val[i] - val[7 - i]) for i in range(4)]
-                coef = cb[h, rows, :]
-                for p in range(4):
-                    ev = sum(even[p][i] * plus[i] for i in range(4))
-                    od = sum(odd[p][i] * minus[i] for i in range(4))
-                    w = float(WEIGHTS[p])
-                    d_low = coef * (ev + od + w * yz[h, p, rows, :])
-                    d_high = coef * (ev - od + w * yz[h, 7 - p, rows, :])
-                    db[h, p, rows, :] = d_low
-                    db[h, 7 - p, rows, :] = d_high
-                    if p == 0:
-                        sx[k, 0, h, rows, :] = d_low
-                        sx[k, 1, h, rows, :] = d_high
-                    if e in (0, 7):
-                        side = 0 if e == 0 else 1
-                        j = 0 if e == 0 else 7
-                        sy[k, side, h, p : p + 1, :] = d_low[j : j + 1]
-                        sy[k, side, h, 7 - p : 8 - p, :] = d_high[j : j + 1]
-                        if p == 0:
-                            sd[k, 0, side, h : h + 1, :] = d_low[j : j + 1]
-                            sd[k, 1, side, h : h + 1, :] = d_high[j : j + 1]
+            mine_rows = [(f, n) for q, f, n in parts if q == p]
+            if not mine_rows:
+                continue
+
+            def stack(lanes):
+                pieces = [
+                    jnp.concatenate(
+                        [uz[0, p, pl.ds(f, n), lanes], uz[1, p, pl.ds(f, n), lanes]], axis=1
+                    )
+                    for f, n in mine_rows
+                ]
+                return pieces[0] if len(pieces) == 1 else jnp.concatenate(pieces, axis=0)
+
+            top = stack(slice(0, 128))
+            both = jnp.concatenate([top, stack(slice(128, 256)), top], axis=0)
+            table = many if mine_rows[0][1] == 64 else few
+            out = jnp.dot(table, both, preferred_element_type=F32)
+            at_row = 0
+            for f, n in mine_rows:
+                for h in range(2):
+                    rows = pl.ds(f, n)
+                    piece = out[at_row : at_row + n, h * 128 : h * 128 + 128]
+                    yz[h, p, rows, :] = yz[h, p, rows, :] + piece
+                at_row += n
+
+    def tile(k, h, e, pairs):
+        rows = pl.ds(e * 8, 8)
+        val = [u[h, p, rows, :] for p in range(8)]
+        plus = [(val[i] + val[7 - i]) for i in range(4)]
+        minus = [(val[i] - val[7 - i]) for i in range(4)]
+        coef = cb[h, rows, :]
+        for p in pairs:
+            ev = sum(even[p][i] * plus[i] for i in range(4))
+            od = sum(odd[p][i] * minus[i] for i in range(4))
+            w = float(WEIGHTS[p])
+            d_low = coef * (ev + od + w * yz[h, p, rows, :])
+            d_high = coef * (ev - od + w * yz[h, 7 - p, rows, :])
+            db[h, p, rows, :] = d_low
+            db[h, 7 - p, rows, :] = d_high
+            if p == 0:
+                sx[k, 0, h, rows, :] = d_low
+                sx[k, 1, h, rows, :] = d_high
+            if e in (0, 7):
+                side = 0 if e == 0 else 1
+                j = 0 if e == 0 else 7
+                sy[k, side, h, p : p + 1, :] = d_low[j : j + 1]
+                sy[k, side, h, 7 - p : 8 - p, :] = d_high[j : j + 1]
+                if p == 0:
+                    sd[k, 0, side, h : h + 1, :] = d_low[j : j + 1]
+                    sd[k, 1, side, h : h + 1, :] = d_high[j : j + 1]
 
     def messages(k):
         ss = sends.at[k]
@@ -470,54 +503,58 @@
             remote(sx.at[k, 1], rx.at[k, 1], ss.at[1], rs.at[1], at(0, 0, other)),
         ]
 
-    def assemble(k):
+    def rows_of_round(k, side):
+        raw = []
+        for h in range(2):
+            d = ry[k, side, h]
+            d = d + jnp.where(row == 0, spread_rows(rd[k, 0, side, h : h + 1, :]), 0.0)
+            d = d + jnp.where(row == 7, spread_rows(rd[k, 1, side, h : h + 1, :]), 0.0)
+            raw.append(d)
+        return z_sum(*raw)
+
+    sent = list(first)
+    norms = []
+    total = update(0, "inner")
+    multiply("inner")
+    for k in range(ROUNDS):
+        total = total + update(k, "outer")
+        multiply("outer")
+        for h in range(2):
+            for e in (0, 7):
+                tile(k, h, e, range(4))
+            for e in range(1, 7):
+                tile(k, h, e, (0,))
         copies = messages(k)
         for copy in copies:
             copy.start()
-        for p in range(1, 7):
-            db[0, p], db[1, p] = z_sum(db[0, p], db[1, p])
-        y_own(range(1, 7))
+        sent += copies
+        if k % 2 == 0:
+            norms.append(norm_of(total))
         if k == ROUNDS - 1:
-            for p in range(8):
-                out_ref[8 * t + p] = sol[t, p]
-        for copy in copies:
-            copy.wait_recv()
-        for side, p in ((0, 0), (1, 7)):
-            db[0, p], db[1, p] = z_sum(
-                db[0, p] + rx[k, side, 0], db[1, p] + rx[k, side, 1]
-            )
-
-        def rows_of(side):
-            raw = []
-            for h in range(2):
-                d = ry[k, side, h]
-                d = d + jnp.where(row == 0, spread_rows(rd[k, 0, side, h : h + 1, :]), 0.0)
-                d = d + jnp.where(row == 7, spread_rows(rd[k, 1, side, h : h + 1, :]), 0.0)
-                raw.append(d)
-            return z_sum(*raw)
-
-        y_own((0, 7))
-        y_add(rows_of)
-        return copies
-
-    sent = list(first)
-    norms = []
-    tail = []
-    for step in range(ROUNDS):
-        total = update(step)
-        if step % 2 == 0:
-            norms.append(norm_of(total))
-        if step == ROUNDS - 1:
             half_rows = pl.ds(8 * t, 8)
             away = remote(
                 sol.at[other], out_ref.at[half_rows], out_send, out_recv, at(0, 0, other)
             )
             away.start()
-            tail = [away]
-        apply(step)
-        sent += assemble(step)
-        reach_step(step + 2)
-    norms.append(norm_of(update(ROUNDS)))
+            for p in range(8):
+                out_ref[8 * t + p] = sol[t, p]
+        for h in range(2):
+            for e in range(1, 7):
+                tile(k, h, e, (1, 2, 3))
+        for p in range(1, 7):
+            db[0, p], db[1, p] = z_sum(db[0, p], db[1, p])
+        y_own(range(1, 7))
+        total = update(k + 1, "inner")
+        if k < ROUNDS - 1:
+            multiply("inner")
+        for copy in copies:
+            copy.wait_recv()
+        for side, p in ((0, 0), (1, 7)):
+            db[0, p], db[1, p] = z_sum(db[0, p] + rx[k, side, 0], db[1, p] + rx[k, side, 1])
+        y_own((0, 7))
+        y_add(lambda side: rows_of_round(k, side))
+        reach_step(k + 2)
+    norms.append(norm_of(total + update(ROUNDS, "outer")))
 
     lane1 = lax.broadcasted_iota(jnp.int32, (1, 128), 1)
     line = jnp.where(lane1 == 0, norms[0], jnp.where(lane1 == 1, norms[1], norms[2]))
@@ -527,6 +564,8 @@
         hops.append(remote(v1, a1.at[gy], s1_sem.at[o], r1_sem.at[gy], at(0, o, t)))
     for copy in hops:
         copy.start()
+    for copy in sent:
+        copy.wait_send()
     a1[gy] = line
     for o in range(1, ny):
         source = lax.rem(gy + o, ny)
@@ -544,6 +583,9 @@
             wide.append(remote(v2, a2.at[slot], s2_sem.at[i], r2_sem.at[slot], at(o, 0, core)))
     for copy in wide:
         copy.start()
+    for copy in hops + [away]:
+        copy.wait_send()
+    away.wait_recv()
     a2[slot] = line
     for o in range(0, nx):
         for flip in range(2):
@@ -553,10 +595,11 @@
             wait_for(a2.at[source], r2_sem.at[source])
     line = jnp.sum(a2[...], axis=0)
     whole = line[0, 0]
-    ratio_ref[...] = pltpu.roll(jnp.sqrt(line / whole), 127, 1)[:, 0:2]
-
-    tail[0].wait_recv()
-    for copy in sent + hops + wide + tail[:1]:
+    ratios = jnp.sqrt(line / whole)
+    ratio_ref[0] = ratios[0, 1]
+    ratio_ref[1] = ratios[0, 2]
+
+    for copy in wide:
         copy.wait_send()
 
 
@@ -578,7 +621,7 @@
         vmem(2, 8, 64, 128),
         pltpu.VMEM((2, 8, 64, 256), BF16),
         vmem(2, 8, 64, 128),
-        pltpu.VMEM((320, 256), BF16),
+        pltpu.VMEM((352, 256), BF16),
         vmem(88, 128),
         vmem(ROUNDS, 2, 2, 64, 128),
         vmem(ROUNDS, 2, 2, 64, 128),
@@ -609,14 +652,15 @@
     ]
     anywhere = pl.BlockSpec(memory_space=pl.ANY)
     in_vmem = pl.BlockSpec(memory_space=pltpu.VMEM)
+    in_smem = pl.BlockSpec(memory_space=pltpu.SMEM)
     result, line = pl.pallas_call(
         functools.partial(smoother, nx, ny),
         out_shape=(
             pltpu.VMEM(forcing.shape, F32),
-            jax.ShapeDtypeStruct((1, 2), F32),
+            pltpu.SMEM((2,), F32),
         ),
         in_specs=[anywhere] * 6,
-        out_specs=(in_vmem, in_vmem),
+        out_specs=(in_vmem, in_smem),
         scratch_shapes=scratch,
         compiler_params=pltpu.CompilerParams(collective_id=0, has_side_effects=True),
     )(
@@ -627,7 +671,7 @@
         jnp.asarray(bf16_tables(), BF16),
         jnp.asarray(f32_tables(), F32),
     )
-    return result, line.reshape(2)
+    return result, line
 
 
 def solution(mesh):

time: 60.9 us -> 59 us (0.969)
  Pallas kernels: 56.9 us -> 55.6 us
  local copies, waits for them, and re-layouts: 1.93 us -> 1.31 us
    pallas_call x1, Pallas kernels: 56.9 us -> 55.6 us  [per_device(): pl.pallas_call(functools.partial(smoother, nx, ny), out_shape=(pltpu.VMEM...]
    unnamed x4 -> x2, local copies, waits for them, and re-layouts: 1.93 us -> 1.31 us
where the time goes in v3:
time: 59 us; the launch traced here: 58.8 us
  Pallas kernels  55.6 us (94%)
  between operations  1.93 us (3%)
  local copies, waits for them, and re-layouts  1.31 us (2%)
    pallas_call x1, Pallas kernels, per_device(): pl.pallas_call(functools.partial(smoother, nx, ny), out_shape=(pltpu.VMEM...  55.6 us
    unnamed x2, local copies, waits for them, and re-layouts  1.31 us

profile of v3, /device:TPU:1, one launch (start us, length us, event | category | flops | bytes accessed | tf_op | source)
XLA Modules:
  0.0 58.8 jit_solution(5410763254716324515)
XLA Ops:
  1.9 55.6 %shard_map.77 = (f32[16,64,128]{2,1,0:T(8,128)S(1)}, f32[2]{0:T(128)S(4)}) custom-call(f32[16,64,128]{2,1,0:T(8,128)} %f_ref.1, f32[2,8,16]{2,1,0:T(8,128)} %c_ref.1, f32[1]{0:T(128)S(6)} %copy.12.lo_ref, f32[1]{0:T(128)S(6)} %copy.13.up_ref, bf16[352,256]{1,0:T(8,128)(2,1)} %constant.4.clone.kb_ref, f32[88,128]{1,0:T(8,128)} %constant.5.clone.kf_ref), custom_call_target="tpu_custom_call" | custom-call | tf_op jit(solution)/shard_map/pallas_call | solution.py:656
  57.5 0.8 %copy.10 = f32[16,64,128]{2,1,0:T(8,128)} copy(f32[16,64,128]{2,1,0:T(8,128)S(1)} %get-tuple-element.2) | data formatting | bytes 1048576
  58.3 0.5 copy.11

commit v4 on v3

--- a/solution.py
+++ b/solution.py
@@ -310,75 +310,6 @@
                 db[h, p, 0:1, :] = db[h, p, 0:1, :] + low_rows[h][one]
                 db[h, p, 63:64, :] = db[h, p, 63:64, :] + high_rows[h][one]
 
-    other = 1 - t
-    weight_jk = kf[16:24, :]
-    wait_for(fb.at[other, theirs], recv0.at[0])
-    own_c = [fb[h, plane(0), 64:72, :] for h in range(2)]
-    int_c = [fb[h, plane(8), 64:72, :] for h in range(2)]
-    for h in range(2):
-        for e in range(8):
-            cb[h, e * 8 : e * 8 + 8, :] = spread_rows(own_c[h][e : e + 1]) * weight_jk
-    for p in range(1, 7):
-        db[0, p], db[1, p] = z_sum(fb[0, plane(p), 0:64, :], fb[1, plane(p), 0:64, :])
-    y_own(range(1, 7))
-    db[0, 7], db[1, 7] = z_sum(
-        *[fb[h, plane(7), 0:64, :] + fb[h, plane(8), 0:64, :] for h in range(2)]
-    )
-    for h in range(2):
-        wait_for(xe0.at[h], recv0.at[1 + h])
-        for side in range(2):
-            wait_for(y0.at[side, h], recv0.at[3 + 2 * side + h])
-            wait_for(xy0.at[side, h], recv0.at[7 + 2 * side + h])
-    db[0, 0], db[1, 0] = z_sum(
-        *[fb[h, plane(0), 0:64, :] + xe0[h, 0:64, :] for h in range(2)]
-    )
-
-    def first_rows(side):
-        raw = []
-        for h in range(2):
-            d = y0[side, h, 0:8, :]
-            d = d + jnp.where(row == 0, spread_rows(xy0[side, h, 0:1, :]), 0.0)
-            d = d + jnp.where(row == 7, spread_rows(y0[side, h, 8:9, :]), 0.0)
-            raw.append(d)
-        return z_sum(*raw)
-
-    y_own((0, 7))
-    y_add(first_rows)
-
-    for variant in range(3):
-        own = own_c
-        near = [[spread_rows(y0[s, h, 9:10, :]) for h in range(2)] for s in range(2)]
-        if variant == 1:
-            own = [own[h] + xe0[h, 64:72, :] for h in range(2)]
-            near = [
-                [near[s][h] + spread_rows(xy0[s, h, 9:10, :]) for h in range(2)] for s in range(2)
-            ]
-        if variant == 2:
-            own = [own[h] + int_c[h] for h in range(2)]
-            near = [
-                [near[s][h] + spread_rows(y0[s, h, 10:11, :]) for h in range(2)] for s in range(2)
-            ]
-        own = z_sum(*own)
-        near = [z_sum(*pair) for pair in near]
-        for h in range(2):
-            a = own[h] + jnp.where(row == 7, near[1][h], pltpu.roll(own[h], 7, 0))
-            b = own[h] + jnp.where(row == 0, near[0][h], pltpu.roll(own[h], 1, 0))
-            for e in range(8):
-                one = slice(e, e + 1)
-                tile = jnp.where(
-                    row == 7,
-                    spread_rows(a[one]),
-                    jnp.where(row == 0, spread_rows(b[one]), spread_rows(own[h][one])),
-                )
-                flip = bound[h, e] / tile
-                if variant == 1:
-                    flip = flip * inner_x
-                for p in {0: range(1, 7), 1: (0,), 2: (7,)}[variant]:
-                    inv[h, p, e * 8 : e * 8 + 8, :] = flip * kf[24 + 8 * p : 32 + 8 * p, :]
-
-    reach_step(1)
-    loads[2].wait()
-
     stiff = STIFF
     even = [[float(stiff[p, i] + stiff[p, 7 - i]) / 2 for i in range(4)] for p in range(4)]
     odd = [[float(stiff[p, i] - stiff[p, 7 - i]) / 2 for i in range(4)] for p in range(4)]
@@ -488,6 +419,77 @@
                     sd[k, 0, side, h : h + 1, :] = d_low[j : j + 1]
                     sd[k, 1, side, h : h + 1, :] = d_high[j : j + 1]
 
+    def inverse_tiles(own, near, planes, elements, scale):
+        for h in range(2):
+            up, down = pltpu.roll(own[h], 7, 0), pltpu.roll(own[h], 1, 0)
+            if near is not None:
+                up = jnp.where(row == 7, near[1][h], up)
+                down = jnp.where(row == 0, near[0][h], down)
+            a, b = own[h] + up, own[h] + down
+            for e in elements:
+                one = slice(e, e + 1)
+                ends = jnp.where(
+                    row == 0, spread_rows(b[one]), spread_rows(own[h][one])
+                )
+                flip = bound[h, e] * scale / jnp.where(row == 7, spread_rows(a[one]), ends)
+                for p in planes:
+                    inv[h, p, e * 8 : e * 8 + 8, :] = flip * kf[24 + 8 * p : 32 + 8 * p, :]
+
+    other = 1 - t
+    weight_jk = kf[16:24, :]
+    wait_for(fb.at[other, theirs], recv0.at[0])
+    own_c = [fb[h, plane(0), 64:72, :] for h in range(2)]
+    int_c = [fb[h, plane(8), 64:72, :] for h in range(2)]
+    for h in range(2):
+        for e in range(8):
+            cb[h, e * 8 : e * 8 + 8, :] = spread_rows(own_c[h][e : e + 1]) * weight_jk
+    for p in range(1, 7):
+        db[0, p], db[1, p] = z_sum(fb[0, plane(p), 0:64, :], fb[1, plane(p), 0:64, :])
+    y_own(range(1, 7))
+    own_z = z_sum(*own_c)
+    inverse_tiles(own_z, None, range(1, 7), range(1, 7), 1.0)
+    loads[2].wait()
+    total = update(0, "inner")
+    multiply("inner")
+    db[0, 7], db[1, 7] = z_sum(
+        *[fb[h, plane(7), 0:64, :] + fb[h, plane(8), 0:64, :] for h in range(2)]
+    )
+    for h in range(2):
+        wait_for(xe0.at[h], recv0.at[1 + h])
+        for side in range(2):
+            wait_for(y0.at[side, h], recv0.at[3 + 2 * side + h])
+            wait_for(xy0.at[side, h], recv0.at[7 + 2 * side + h])
+    db[0, 0], db[1, 0] = z_sum(
+        *[fb[h, plane(0), 0:64, :] + xe0[h, 0:64, :] for h in range(2)]
+    )
+
+    def first_rows(side):
+        raw = []
+        for h in range(2):
+            d = y0[side, h, 0:8, :]
+            d = d + jnp.where(row == 0, spread_rows(xy0[side, h, 0:1, :]), 0.0)
+            d = d + jnp.where(row == 7, spread_rows(y0[side, h, 8:9, :]), 0.0)
+            raw.append(d)
+        return z_sum(*raw)
+
+    y_own((0, 7))
+    y_add(first_rows)
+
+    near_c = [[spread_rows(y0[s, h, 9:10, :]) for h in range(2)] for s in range(2)]
+    inverse_tiles(own_z, [z_sum(*pair) for pair in near_c], range(1, 7), (0, 7), 1.0)
+    ext_near = [
+        z_sum(*[near_c[s][h] + spread_rows(xy0[s, h, 9:10, :]) for h in range(2)])
+        for s in range(2)
+    ]
+    ext_own = z_sum(*[own_c[h] + xe0[h, 64:72, :] for h in range(2)])
+    inverse_tiles(ext_own, ext_near, (0,), range(8), inner_x)
+    int_near = [
+        z_sum(*[near_c[s][h] + spread_rows(y0[s, h, 10:11, :]) for h in range(2)])
+        for s in range(2)
+    ]
+    int_own = z_sum(*[own_c[h] + int_c[h] for h in range(2)])
+    inverse_tiles(int_own, int_near, (7,), range(8), 1.0)
+
     def messages(k):
         ss = sends.at[k]
         rs = recvs.at[k]
@@ -495,11 +497,11 @@
         return [
             remote(sd.at[k, 0, 0], rd.at[k, 0, 1], ss.at[4], rs.at[5], at(ext, -1, other)),
             remote(sd.at[k, 0, 1], rd.at[k, 0, 0], ss.at[5], rs.at[4], at(ext, 1, other)),
-            remote(sx.at[k, 0], rx.at[k, 0], ss.at[0], rs.at[0], at(ext, 0, other)),
             remote(sd.at[k, 1, 0], rd.at[k, 1, 1], ss.at[6], rs.at[7], at(0, -1, other)),
             remote(sd.at[k, 1, 1], rd.at[k, 1, 0], ss.at[7], rs.at[6], at(0, 1, other)),
             remote(sy.at[k, 0], ry.at[k, 1], ss.at[2], rs.at[3], at(0, -1, t)),
             remote(sy.at[k, 1], ry.at[k, 0], ss.at[3], rs.at[2], at(0, 1, t)),
+            remote(sx.at[k, 0], rx.at[k, 0], ss.at[0], rs.at[0], at(ext, 0, other)),
             remote(sx.at[k, 1], rx.at[k, 1], ss.at[1], rs.at[1], at(0, 0, other)),
         ]
 
@@ -514,20 +516,22 @@
 
     sent = list(first)
     norms = []
-    total = update(0, "inner")
-    multiply("inner")
     for k in range(ROUNDS):
         total = total + update(k, "outer")
         multiply("outer")
+        copies = messages(k)
         for h in range(2):
             for e in (0, 7):
                 tile(k, h, e, range(4))
+        for copy in copies[:6]:
+            copy.start()
+        for h in range(2):
             for e in range(1, 7):
                 tile(k, h, e, (0,))
-        copies = messages(k)
-        for copy in copies:
+        for copy in copies[6:]:
             copy.start()
         sent += copies
+        reach_step(k + 1)
         if k % 2 == 0:
             norms.append(norm_of(total))
         if k == ROUNDS - 1:
@@ -553,14 +557,13 @@
             db[0, p], db[1, p] = z_sum(db[0, p] + rx[k, side, 0], db[1, p] + rx[k, side, 1])
         y_own((0, 7))
         y_add(lambda side: rows_of_round(k, side))
-        reach_step(k + 2)
     norms.append(norm_of(total + update(ROUNDS, "outer")))
 
     lane1 = lax.broadcasted_iota(jnp.int32, (1, 128), 1)
     line = jnp.where(lane1 == 0, norms[0], jnp.where(lane1 == 1, norms[1], norms[2]))
     v1[...] = line
     hops = []
-    for o in range(1, ny):
+    for o in sorted(range(1, ny), key=lambda o: -min(o, ny - o)):
         hops.append(remote(v1, a1.at[gy], s1_sem.at[o], r1_sem.at[gy], at(0, o, t)))
     for copy in hops:
         copy.start()

time: 59 us -> 58.5 us (level)
  no operation moved by 1% of the time
where the time goes in v4:
time: 58.5 us; the launch traced here: 58.3 us
  Pallas kernels  55.1 us (94%)
  between operations  1.93 us (3%)
  local copies, waits for them, and re-layouts  1.31 us (2%)
    pallas_call x1, Pallas kernels, per_device(): pl.pallas_call(functools.partial(smoother, nx, ny), out_shape=(pltpu.VMEM...  55.1 us
    unnamed x2, local copies, waits for them, and re-layouts  1.31 us

profile of v4, /device:TPU:1, one launch (start us, length us, event | category | flops | bytes accessed | tf_op | source)
XLA Modules:
  0.0 58.3 jit_solution(966193449132998715)
XLA Ops:
  1.9 55.1 %shard_map.77 = (f32[16,64,128]{2,1,0:T(8,128)S(1)}, f32[2]{0:T(128)S(4)}) custom-call(f32[16,64,128]{2,1,0:T(8,128)} %f_ref.1, f32[2,8,16]{2,1,0:T(8,128)} %c_ref.1, f32[1]{0:T(128)S(6)} %copy.12.lo_ref, f32[1]{0:T(128)S(6)} %copy.13.up_ref, bf16[352,256]{1,0:T(8,128)(2,1)} %constant.4.clone.kb_ref, f32[88,128]{1,0:T(8,128)} %constant.5.clone.kf_ref), custom_call_target="tpu_custom_call" | custom-call | tf_op jit(solution)/shard_map/pallas_call | solution.py:659
  57.0 0.8 %copy.10 = f32[16,64,128]{2,1,0:T(8,128)} copy(f32[16,64,128]{2,1,0:T(8,128)S(1)} %get-tuple-element.2) | data formatting | bytes 1048576
  57.8 0.5 copy.11

commit v5 on v4

--- a/solution.py
+++ b/solution.py
@@ -323,6 +323,15 @@
         + [(p, first, 16) for p in range(1, 7) for first in (0, 48)],
     }
 
+    def square_of(res, h, p, rows, n):
+        square = res * res * wn[h, rows, :]
+        part = jnp.sum(square.reshape(n // 8, 8, 128), axis=0)
+        if p == 0:
+            part = part * (0.5 * inner_x)
+        if p == 7:
+            part = part * 0.5
+        return part
+
     def update(step, region):
         total = jnp.zeros((8, 128), F32)
         for h in range(2):
@@ -331,14 +340,8 @@
                 res = db[h, p, rows, :]
                 if step > 0:
                     res = r[h, p, rows, :] - res
-                if step % 2 == 0:
-                    square = res * res * wn[h, rows, :]
-                    part = jnp.sum(square.reshape(n // 8, 8, 128), axis=0)
-                    if p == 0:
-                        part = part * (0.5 * inner_x)
-                    if p == 7:
-                        part = part * 0.5
-                    total = total + part
+                if step == ROUNDS or (step % 2 == 0 and region == "inner"):
+                    total = total + square_of(res, h, p, rows, n)
                 if step == ROUNDS:
                     continue
                 r[h, p, rows, :] = res
@@ -533,6 +536,10 @@
         sent += copies
         reach_step(k + 1)
         if k % 2 == 0:
+            for h in range(2):
+                for p, first_row, n in regions["outer"]:
+                    rows = pl.ds(first_row, n)
+                    total = total + square_of(r[h, p, rows, :], h, p, rows, n)
             norms.append(norm_of(total))
         if k == ROUNDS - 1:
             half_rows = pl.ds(8 * t, 8)
@@ -577,8 +584,11 @@
     v2[...] = line
     slot = gx * 2 + t
     wide = []
-    for o in range(0, nx):
-        for flip in range(2):
+    far_first = sorted(
+        range(nx), key=lambda o: -min(o % 4, 4 - o % 4) - min(o // 4, 4 - o // 4)
+    )
+    for o in far_first:
+        for flip in (1, 0):
             if o == 0 and flip == 0:
                 continue
             core = other if flip else t

time: 58.5 us -> 58.6 us (level)
  no operation moved by 1% of the time
where the time goes in v5:
time: 58.6 us; the launch traced here: 58.4 us
  Pallas kernels  55.2 us (94%)
  between operations  1.93 us (3%)
  local copies, waits for them, and re-layouts  1.31 us (2%)
    pallas_call x1, Pallas kernels, per_device(): pl.pallas_call(functools.partial(smoother, nx, ny), out_shape=(pltpu.VMEM...  55.2 us
    unnamed x2, local copies, waits for them, and re-layouts  1.31 us

profile of v5, /device:TPU:1, one launch (start us, length us, event | category | flops | bytes accessed | tf_op | source)
XLA Modules:
  0.0 58.4 jit_solution(14191679820813640847)
XLA Ops:
  1.9 55.2 %shard_map.77 = (f32[16,64,128]{2,1,0:T(8,128)S(1)}, f32[2]{0:T(128)S(4)}) custom-call(f32[16,64,128]{2,1,0:T(8,128)} %f_ref.1, f32[2,8,16]{2,1,0:T(8,128)} %c_ref.1, f32[1]{0:T(128)S(6)} %copy.12.lo_ref, f32[1]{0:T(128)S(6)} %copy.13.up_ref, bf16[352,256]{1,0:T(8,128)(2,1)} %constant.4.clone.kb_ref, f32[88,128]{1,0:T(8,128)} %constant.5.clone.kf_ref), custom_call_target="tpu_custom_call" | custom-call | tf_op jit(solution)/shard_map/pallas_call | solution.py:669
  57.1 0.8 %copy.10 = f32[16,64,128]{2,1,0:T(8,128)} copy(f32[16,64,128]{2,1,0:T(8,128)S(1)} %get-tuple-element.2) | data formatting | bytes 1048576
  57.9 0.5 copy.11
